TPU v7x, 256 devices: a whole 4x4x8 slice. The times are simulated.
256 devices in a mesh: curve: 64 (over y, z, core), sub: 4 (over x).
Axes of the slice: x: 4, y: 4, z: 8, core: 2. Of those that a mesh axis runs over, the one named last changes fastest.
Arguments:
- forcing: float32 [12, 6144, 1024], P(None, 'curve', 'sub'), may hold values from -10 to 10
- metric: float32 [6144, 1024], P('curve', 'sub'), may hold values from 0.25 to 4
- jacobian: float32 [6144, 1024], P('curve', 'sub'), may hold values from 0.5 to 2
- mode_scale: float32 [12], replicated, may hold values from 0.1 to 10
Outputs:
- solution: float32 [12, 6144, 1024], P(None, 'curve', 'sub')
- residual: float32 [12, 6144, 1024], P(None, 'curve', 'sub')
All inputs are finite; a program needn't handle non-finite values.
Results may differ from a plain program's by a relative error of at most 0.0003.
Values sent between devices are 32-bit elements; how exact they have to be, the bound alone decides.
A program may use at most 64 MiB of HBM per device.

v0:
```python
import functools
import math

import jax
import jax.numpy as jnp
import numpy as np
from jax import lax
from jax.sharding import Mesh
from jax.sharding import PartitionSpec as P

ITERS = 3
CURVE_SUB = ("curve_0", "curve_1", "curve_2", "sub")
CURVE = ("curve_0", "curve_1", "curve_2")


def extended(cells, sides, width):
    for axis, dim in sides:
        count = lax.axis_size(axis)
        head = lax.slice_in_dim(cells, 0, width, axis=dim)
        tail = lax.slice_in_dim(cells, cells.shape[dim] - width, cells.shape[dim], axis=dim)
        cells = jnp.concatenate(
            [
                lax.ppermute(tail, axis, [(i, (i + 1) % count) for i in range(count)]),
                cells,
                lax.ppermute(head, axis, [((i + 1) % count, i) for i in range(count)]),
            ],
            axis=dim,
        )
    return cells


def one_axis_at_a_time(x, axes):
    return functools.reduce(lax.psum, axes, x)


def gll_tables():
    points = np.array([-1.0, -1.0 / math.sqrt(5.0), 1.0 / math.sqrt(5.0), 1.0])
    weights = np.array([1.0 / 6.0, 5.0 / 6.0, 5.0 / 6.0, 1.0 / 6.0])
    factor = np.array(
        [np.prod([points[j] - points[m] for m in range(4) if m != j]) for j in range(4)]
    )
    slopes = np.zeros((4, 4))
    for i in range(4):
        for j in range(4):
            if i != j:
                slopes[i, j] = factor[i] / (factor[j] * (points[i] - points[j]))
        slopes[i, i] = sum((1.0 / (points[i] - points[m]) for m in range(4) if m != i))
    return (slopes, weights)


def line_tables(count):
    phase = jnp.arange(count, dtype=jnp.int32) % 4
    on_edge = (phase == 0) | (phase == 3)
    line_w = jnp.where(on_edge, jnp.float32(1.0 / 6.0), jnp.float32(5.0 / 6.0))
    line_mult = jnp.where(on_edge, jnp.float32(2.0), jnp.float32(1.0))
    return (line_w, line_mult)


def combine(padded, axis_dim):
    length = padded.shape[axis_dim] - 2
    center = lax.slice_in_dim(padded, 1, length + 1, axis=axis_dim)
    next_row = lax.slice_in_dim(padded, 2, length + 2, axis=axis_dim)
    before = lax.slice_in_dim(padded, 0, length, axis=axis_dim)
    phase = lax.broadcasted_iota(jnp.int32, center.shape, axis_dim) % 4
    return center + jnp.where(phase == 3, next_row, 0.0) + jnp.where(phase == 0, before, 0.0)


def assemble(values):
    padded = extended(values, ((CURVE, 1), ("sub", 2)), 1)
    return combine(combine(padded, 1), 2)


def along_rows(table, values):
    mode_count, row_count, col_count = values.shape
    shaped = values.reshape(mode_count, row_count // 4, 4, col_count)
    result = jnp.einsum("ka,mxkc->mxac", table, shaped, precision=lax.Precision.HIGHEST)
    return result.reshape(mode_count, row_count, col_count)


def along_cols(table, values):
    lead = values.shape[:-1]
    col_count = values.shape[-1]
    shaped = values.reshape(lead + (col_count // 128, 128))
    result = jnp.matmul(shaped, table, precision=lax.Precision.HIGHEST)
    return result.reshape(lead + (col_count,))


def shards(forcing, metric, jacobian, mode_scale):
    slopes_np = gll_tables()[0]
    slopes = jnp.asarray(slopes_np, jnp.float32)
    col_block = jnp.asarray(np.kron(np.eye(32), slopes_np), jnp.float32)
    col_block_t = jnp.transpose(col_block)
    squared = slopes * slopes
    col_squared = col_block * col_block
    row_w, row_mult = line_tables(metric.shape[0])
    col_w, col_mult = line_tables(metric.shape[1])
    grid_w = row_w[:, None] * col_w[None, :]
    inv_count = (1.0 / (row_mult[:, None] * col_mult[None, :]))[None]
    mass_w = jacobian * grid_w
    flux_w = metric * grid_w
    scale3 = mode_scale[:, None, None]
    mode_count = forcing.shape[0]

    def inner(left, right):
        return jnp.sum(left * right * inv_count, axis=(1, 2))

    lap_terms = along_rows(squared, flux_w[None])[0] + along_cols(col_squared, flux_w)
    stacked = jnp.concatenate([forcing * mass_w[None], mass_w[None], lap_terms[None]], axis=0)
    assembled = assemble(stacked)
    rhs = assembled[:mode_count]
    precond = assembled[mode_count][None] + scale3 * assembled[mode_count + 1][None]
    solution = jnp.zeros_like(rhs)
    residual = rhs
    direction = jnp.zeros_like(rhs)
    along = jnp.zeros_like(rhs)
    rho_old = jnp.ones((mode_count,), jnp.float32)
    step_old = jnp.ones((mode_count,), jnp.float32)
    for iteration in range(ITERS):
        zvec = residual / precond
        grad_x = along_rows(jnp.transpose(slopes), zvec)
        grad_y = along_cols(col_block_t, zvec)
        lap = along_rows(slopes, flux_w[None] * grad_x) + along_cols(
            col_block, flux_w[None] * grad_y
        )
        image = assemble(mass_w[None] * zvec + scale3 * lap)
        rho_next, curve_sum = (
            one_axis_at_a_time(inner(residual, zvec), CURVE_SUB),
            one_axis_at_a_time(inner(image, zvec), CURVE_SUB),
        )
        if iteration == 0:
            step_len = rho_next / curve_sum
            direction = zvec
            along = image
        else:
            mixing = rho_next / rho_old
            step_len = rho_next / (curve_sum - mixing * rho_next / step_old)
            direction = zvec + mixing[:, None, None] * direction
            along = image + mixing[:, None, None] * along
        solution = solution + step_len[:, None, None] * direction
        residual = residual - step_len[:, None, None] * along
        rho_old = rho_next
        step_old = step_len
    return (solution, residual)


def solution(mesh):
    torus = Mesh(
        mesh.devices.reshape(4, 8, 2, mesh.shape["sub"]), ("curve_0", "curve_1", "curve_2", "sub")
    )
    in_specs = (P(None, CURVE, "sub"), P(CURVE, "sub"), P(CURVE, "sub"), P())
    out_specs = (P(None, CURVE, "sub"), P(None, CURVE, "sub"))
    return jax.shard_map(
        shards, mesh=torus, in_specs=in_specs, out_specs=out_specs, check_vma=False
    )
```

profile of v0, /device:TPU:40, one launch (start us, length us, event | category | flops | bytes accessed | tf_op | source)
XLA Modules:
  0.0 263.6 jit_solution(1248867511350576800)
XLA Ops:
  3.7 1.7 collective-permute-start.1
  7.1 1.3 fusion.54
  8.4 1.4 copy.18
  10.1 2.8 %collective-permute-start.3 = (f32[14,98,1]{1,2,0:T(1,128)S(1)}, f32[14,98,1]{1,2,0:T(1,128)S(1)}, u32[]{:S(2)}, u32[]{:S(2)}) collective-permute-start(f32[14,98,1]{1,2,0:T(1,128)S(1)} %copy.19), channel_id=1, source_target_pairs={{1,0},{2,1},{3,2},{0,3},{5,4},{6,5},{7,6},{4,7},{9,8},{10,9},{11,1... | collective-permute-start | bytes 16472 | tf_op jit(solution)/shard_map/ppermute | solution.py:25
  13.1 4.8 %collective-permute-done.2 = f32[14,98,1]{1,2,0:T(1,128)S(1)} collective-permute-done((f32[14,98,1]{1,2,0:T(1,128)S(1)}, f32[14,98,1]{1,2,0:T(1,128)S(1)}, u32[]{:S(2)}, u32[]{:S(2)}) %collective-permute-start.2) | collective-permute-done | bytes 5520 | tf_op jit(solution)/shard_map/ppermute | solution.py:23
  22.0 1.2 convolution_multiply_fusion.2
  23.2 2.1 convolution_bitcast_fusion.6
  25.3 1.4 reshape.158
  26.6 3.4 %fusion.16 = f32[12,24,4,256]{3,2,1,0:T(4,128)S(1)} fusion(f32[12,24,4,256]{3,2,1,0:T(4,128)} %reshape.158, f32[4,4,1,1]{1,0,3,2:T(4,128)S(1)} %copy-done.15, f32[24,4,256]{2,1,0:T(4,128)S(1)} %reshape.155), kind=kOutput, calls=%fused_computation.40 | convolution fusion | flops 14450688 | bytes 2457664 | tf_op jit(solution)/shard_map/ka,mxkc->mxac/dot_general | solution.py:76
  30.0 2.2 convolution_bitcast_fusion.7
  32.2 1.4 reshape.159
  33.6 2.0 fusion.36
  36.3 1.4 collective-permute-start.5
  41.2 1.9 copy.26
  44.0 2.0 collective-permute-start.6
  46.0 1.4 multiply_divide_fusion
  47.4 1.7 collective-permute-done.6
  50.1 1.8 copy.29
  52.0 1.9 pad_maximum_fusion.1
  54.8 1.9 multiply_reduce_fusion.4
  56.7 8.7 %all-reduce.8 = (f32[12]{0:T(128)S(1)}, f32[12]{0:T(128)S(1)}) all-reduce(f32[12]{0:T(128)S(1)} %get-tuple-element.7, f32[12]{0:T(128)S(1)} %get-tuple-element.6), channel_id=1, replica_groups=mesh['curve_0'=4,'curve_1'=8,'curve_2'=2,'sub'=4] {'curve_0'}, use_global_device_ids=true, to_apply=%region_1.2 | all-reduce | flops 24 | bytes 192 | tf_op jit(solution)/shard_map/psum | solution.py:33
  65.4 23.1 %all-reduce.2 = (f32[12]{0:T(128)S(1)}, f32[12]{0:T(128)S(1)}) all-reduce(f32[12]{0:T(128)S(1)} %get-tuple-element.24, f32[12]{0:T(128)S(1)} %get-tuple-element.25), channel_id=1, replica_groups=mesh['curve_0'=4,'curve_1'=8,'curve_2'=2,'sub'=4] {'curve_1'}, use_global_device_ids=true, to_apply=%region_2.3 | all-reduce | flops 24 | bytes 192 | tf_op jit(solution)/shard_map/psum | solution.py:33
  88.5 2.5 all-reduce.11
  91.0 9.0 %all-reduce.5 = (f32[12]{0:T(128)S(1)}, f32[12]{0:T(128)S(1)}) all-reduce(f32[12]{0:T(128)S(1)} %get-tuple-element.30, f32[12]{0:T(128)S(1)} %get-tuple-element.31), channel_id=1, replica_groups=mesh['curve_0'=4,'curve_1'=8,'curve_2'=2,'sub'=4] {'sub'}, use_global_device_ids=true, to_apply=%region_4.5 | all-reduce | flops 24 | bytes 192 | tf_op jit(solution)/shard_map/psum | solution.py:33
  100.5 1.7 fusion.48
  103.3 2.1 convolution_bitcast_fusion.3
  105.4 1.2 fusion.44
  106.7 2.6 reshape.162
  109.3 3.4 %fusion.15 = f32[12,24,4,256]{3,2,1,0:T(4,128)S(1)} fusion(f32[12,24,4,256]{3,2,1,0:T(4,128)} %reshape.162, f32[4,4,1,1]{1,0,3,2:T(4,128)S(1)} %copy-done.16, f32[24,4,256]{2,1,0:T(4,128)S(1)} %copy-done.6), kind=kOutput, calls=%fused_computation.36 | convolution fusion | flops 14450688 | bytes 2457664 | tf_op jit(solution)/shard_map/ka,mxkc->mxac/dot_general | solution.py:76
  112.7 3.2 %convolution_bitcast_fusion.4 = f32[12,24,4,256]{3,2,1,0:T(4,128)} fusion(f32[12,24,4,256]{3,2,1,0:T(4,128)S(1)} %fusion.15, f32[4,4,1,1]{1,0,3,2:T(4,128)S(1)} %copy-done.16), kind=kOutput, calls=%fused_computation.34 | convolution fusion | flops 14155776 | bytes 2359360 | tf_op jit(solution)/shard_map/ka,mxkc->mxac/dot_general | solution.py:76
  115.9 2.6 reshape.163
  118.5 2.0 fusion.34
  120.6 1.7 collective-permute-start.9
  122.4 1.4 collective-permute-done.8
  126.2 1.9 copy.33
  128.1 1.2 collective-permute-start.10
  130.1 2.2 collective-permute-start.11
  134.2 1.8 copy.36
  136.1 2.3 pad_maximum_fusion.2
  139.4 1.9 multiply_reduce_fusion.2
  141.3 7.7 %all-reduce.7 = (f32[12]{0:T(128)S(1)}, f32[12]{0:T(128)S(1)}) all-reduce(f32[12]{0:T(128)S(1)} %get-tuple-element.5, f32[12]{0:T(128)S(1)} %get-tuple-element.4), channel_id=1, replica_groups=mesh['curve_0'=4,'curve_1'=8,'curve_2'=2,'sub'=4] {'curve_0'}, use_global_device_ids=true, to_apply=%region_11.12 | all-reduce | flops 24 | bytes 192 | tf_op jit(solution)/shard_map/psum | solution.py:33
  149.0 17.5 %all-reduce.1 = (f32[12]{0:T(128)S(1)}, f32[12]{0:T(128)S(1)}) all-reduce(f32[12]{0:T(128)S(1)} %get-tuple-element.22, f32[12]{0:T(128)S(1)} %get-tuple-element.23), channel_id=1, replica_groups=mesh['curve_0'=4,'curve_1'=8,'curve_2'=2,'sub'=4] {'curve_1'}, use_global_device_ids=true, to_apply=%region_12.13 | all-reduce | flops 24 | bytes 192 | tf_op jit(solution)/shard_map/psum | solution.py:33
  166.4 2.5 all-reduce.10
  168.9 10.9 %all-reduce.4 = (f32[12]{0:T(128)S(1)}, f32[12]{0:T(128)S(1)}) all-reduce(f32[12]{0:T(128)S(1)} %get-tuple-element.28, f32[12]{0:T(128)S(1)} %get-tuple-element.29), channel_id=1, replica_groups=mesh['curve_0'=4,'curve_1'=8,'curve_2'=2,'sub'=4] {'sub'}, use_global_device_ids=true, to_apply=%region_14.15 | all-reduce | flops 24 | bytes 192 | tf_op jit(solution)/shard_map/psum | solution.py:33
  180.4 2.1 fusion.49
  183.7 2.1 convolution_bitcast_fusion
  185.8 1.3 fusion.43
  187.1 2.6 reshape.166
  189.7 3.4 %fusion.14 = f32[12,24,4,256]{3,2,1,0:T(4,128)S(1)} fusion(f32[12,24,4,256]{3,2,1,0:T(4,128)} %reshape.166, f32[4,4,1,1]{1,0,3,2:T(4,128)S(1)} %copy-done.17, f32[24,4,256]{2,1,0:T(4,128)S(1)} %copy-done.7), kind=kOutput, calls=%fused_computation.32 | convolution fusion | flops 14450688 | bytes 2457664 | tf_op jit(solution)/shard_map/ka,mxkc->mxac/dot_general | solution.py:76
  193.1 3.2 %convolution_bitcast_fusion.1 = f32[12,24,4,256]{3,2,1,0:T(4,128)} fusion(f32[12,24,4,256]{3,2,1,0:T(4,128)S(1)} %fusion.14, f32[4,4,1,1]{1,0,3,2:T(4,128)S(1)} %copy-done.17), kind=kOutput, calls=%fused_computation.30 | convolution fusion | flops 14155776 | bytes 2359360 | tf_op jit(solution)/shard_map/ka,mxkc->mxac/dot_general | solution.py:76
  196.3 2.6 %reshape.167 = f32[12,96,256]{2,1,0:T(8,128)} reshape(f32[12,24,4,256]{3,2,1,0:T(4,128)} %convolution_bitcast_fusion.1) | data formatting | bytes 2359296 | tf_op jit(solution)/shard_map/reshape | solution.py:77
  198.9 2.4 fusion.32
  201.6 1.7 collective-permute-start.13
  203.4 1.4 collective-permute-done.12
  206.0 1.3 copy.40
  207.6 3.3 %collective-permute-start.15 = (f32[12,98,1]{1,2,0:T(1,128)S(1)}, f32[12,98,1]{1,2,0:T(1,128)S(1)}, u32[]{:S(2)}, u32[]{:S(2)}) collective-permute-start(f32[12,98,1]{1,2,0:T(1,128)S(1)} %copy.41), channel_id=1, source_target_pairs={{1,0},{2,1},{3,2},{0,3},{5,4},{6,5},{7,6},{4,7},{9,8},{10,9},{11,1... | collective-permute-start | bytes 14120 | tf_op jit(solution)/shard_map/ppermute | solution.py:25
  210.9 1.3 collective-permute-done.14
  213.6 2.3 pad_maximum_fusion.3
  217.3 1.9 multiply_reduce_fusion
  219.2 8.5 %all-reduce.6 = (f32[12]{0:T(128)S(1)}, f32[12]{0:T(128)S(1)}) all-reduce(f32[12]{0:T(128)S(1)} %get-tuple-element.3, f32[12]{0:T(128)S(1)} %get-tuple-element.2), channel_id=1, replica_groups=mesh['curve_0'=4,'curve_1'=8,'curve_2'=2,'sub'=4] {'curve_0'}, use_global_device_ids=true, to_apply=%region_21.22 | all-reduce | flops 24 | bytes 192 | tf_op jit(solution)/shard_map/psum | solution.py:33
  227.7 17.5 %all-reduce = (f32[12]{0:T(128)S(1)}, f32[12]{0:T(128)S(1)}) all-reduce(f32[12]{0:T(128)S(1)} %get-tuple-element.20, f32[12]{0:T(128)S(1)} %get-tuple-element.21), channel_id=1, replica_groups=mesh['curve_0'=4,'curve_1'=8,'curve_2'=2,'sub'=4] {'curve_1'}, use_global_device_ids=true, to_apply=%region_22.23 | all-reduce | flops 24 | bytes 192 | tf_op jit(solution)/shard_map/psum | solution.py:33
  245.2 2.5 all-reduce.9
  247.7 10.9 %all-reduce.3 = (f32[12]{0:T(128)S(1)}, f32[12]{0:T(128)S(1)}) all-reduce(f32[12]{0:T(128)S(1)} %get-tuple-element.26, f32[12]{0:T(128)S(1)} %get-tuple-element.27), channel_id=1, replica_groups=mesh['curve_0'=4,'curve_1'=8,'curve_2'=2,'sub'=4] {'sub'}, use_global_device_ids=true, to_apply=%region_24.25 | all-reduce | flops 24 | bytes 192 | tf_op jit(solution)/shard_map/psum | solution.py:33
  258.6 4.8 %multiply_subtract_fusion = (f32[12,96,256]{2,1,0:T(8,128)}, f32[12,96,256]{2,1,0:T(8,128)}) fusion(f32[12,96,256]{2,1,0:T(8,128)} %copy-done, f32[12,96,256]{2,1,0:T(8,128)} %get-tuple-element.34, f32[12]{0:T(128)S(1)} %get-tuple-element.33, f32[12]{0:T(128)S(1)} %get-tuple-element.32, f32[12,96,256]{2,1,0:T(8,128)} %get-tuple-element.40, ...), kind=kLoop, calls=%fused_computation.78 | loop fusion | flops 5898240 | bytes 9634080 | tf_op jit(solution)/shard_map/sub | solution.py:140
  (198 shorter events, 29.9 us)
Async XLA Ops:
  0.6 2.5 copy-start.54
  0.6 2.9 %copy-start.11 = (f32[12,96,256]{2,1,0:T(8,128)S(1)}, f32[12,96,256]{2,1,0:T(8,128)}, u32[]{:S(2)}) copy-start(f32[12,96,256]{2,1,0:T(8,128)} %param.6) | copy-start | bytes 3538948
  1.8 24.8 %copy-start.5 = (f32[24,4,256]{2,1,0:T(4,128)}, f32[24,4,256]{2,1,0:T(4,128)S(1)}, u32[]{:S(2)}) copy-start(f32[24,4,256]{2,1,0:T(4,128)S(1)} %reshape.155) | copy-start | bytes 294916
  3.6 3.2 %collective-permute-start = (f32[14,1,256]{2,1,0:T(1,128)S(1)}, f32[14,1,256]{2,1,0:T(1,128)S(1)}, u32[]{:S(2)}, u32[]{:S(2)}) collective-permute-start(f32[14,1,256]{2,1,0:T(1,128)S(1)} %get-tuple-element.48), channel_id=1, source_target_pairs={{0,4},{4,8},{8,12},{12,16},{16,20},{20,24},{24,28},{28,32},{32,36}... | collective-permute-start | bytes 43016 | tf_op jit(solution)/shard_map/ppermute | solution.py:23
  3.7 3.2 %collective-permute-start.1 = (f32[14,1,256]{2,1,0:T(1,128)S(1)}, f32[14,1,256]{2,1,0:T(1,128)S(1)}, u32[]{:S(2)}, u32[]{:S(2)}) collective-permute-start(f32[14,1,256]{2,1,0:T(1,128)S(1)} %get-tuple-element.49), channel_id=1, source_target_pairs={{4,0},{8,4},{12,8},{16,12},{20,16},{24,20},{28,24},{32,28},{36,32}... | collective-permute-start | bytes 43016 | tf_op jit(solution)/shard_map/ppermute | solution.py:25
  6.1 13.6 %copy-start.34 = (s32[96]{0:T(128)}, s32[96]{0:T(128)S(1)}, u32[]{:S(2)}) copy-start(s32[96]{0:T(128)S(1)} %get-tuple-element.66) | copy-start | bytes 1156
  6.1 13.6 %copy-start.38 = (s32[96]{0:T(128)}, s32[96]{0:T(128)S(1)}, u32[]{:S(2)}) copy-start(s32[96]{0:T(128)S(1)} %get-tuple-element.67) | copy-start | bytes 1156
  6.1 14.2 %copy-start.26 = (s32[256]{0:T(256)}, s32[256]{0:T(256)S(1)}, u32[]{:S(2)}) copy-start(s32[256]{0:T(256)S(1)} %get-tuple-element.68) | copy-start | bytes 3076
  6.1 14.2 %copy-start.30 = (s32[256]{0:T(256)}, s32[256]{0:T(256)S(1)}, u32[]{:S(2)}) copy-start(s32[256]{0:T(256)S(1)} %get-tuple-element.69) | copy-start | bytes 3076
  6.1 15.3 %copy-start.12 = (f32[96,2,128]{2,0,1:T(8,128)}, f32[96,2,128]{2,0,1:T(8,128)S(1)}, u32[]{:S(2)}) copy-start(f32[96,2,128]{2,0,1:T(8,128)S(1)} %copy_bitcast_fusion) | copy-start | bytes 294916
  6.1 13.5 %copy-start.42 = (pred[96]{0:T(512)(128)(4,1)}, pred[96]{0:T(512)(128)(4,1)S(1)}, u32[]{:S(2)}) copy-start(pred[96]{0:T(512)(128)(4,1)S(1)} %compare_and_fusion.1) | copy-start | bytes 292
  8.4 1.5 copy-start.4
  10.1 8.1 %collective-permute-start.3 = (f32[14,98,1]{1,2,0:T(1,128)S(1)}, f32[14,98,1]{1,2,0:T(1,128)S(1)}, u32[]{:S(2)}, u32[]{:S(2)}) collective-permute-start(f32[14,98,1]{1,2,0:T(1,128)S(1)} %copy.19), channel_id=1, source_target_pairs={{1,0},{2,1},{3,2},{0,3},{5,4},{6,5},{7,6},{4,7},{9,8},{10,9},{11,1... | collective-permute-start | bytes 16472 | tf_op jit(solution)/shard_map/ppermute | solution.py:25
  12.9 5.0 %collective-permute-start.2 = (f32[14,98,1]{1,2,0:T(1,128)S(1)}, f32[14,98,1]{1,2,0:T(1,128)S(1)}, u32[]{:S(2)}, u32[]{:S(2)}) collective-permute-start(f32[14,98,1]{1,2,0:T(1,128)S(1)} %copy.18), channel_id=1, source_target_pairs={{0,1},{1,2},{2,3},{3,0},{4,5},{5,6},{6,7},{7,4},{8,9},{9,10},{10,1... | collective-permute-start | bytes 16472 | tf_op jit(solution)/shard_map/ppermute | solution.py:23
  13.1 7.2 %copy-start.46 = (pred[256]{0:T(512)(128)(4,1)}, pred[256]{0:T(512)(128)(4,1)S(1)}, u32[]{:S(2)}) copy-start(pred[256]{0:T(512)(128)(4,1)S(1)} %compare_and_fusion) | copy-start | bytes 772
  25.3 1.4 copy-start.15
  35.6 3.2 %collective-permute-start.4 = (f32[12,1,256]{2,1,0:T(1,128)S(1)}, f32[12,1,256]{2,1,0:T(1,128)S(1)}, u32[]{:S(2)}, u32[]{:S(2)}) collective-permute-start(f32[12,1,256]{2,1,0:T(1,128)S(1)} %get-tuple-element.62), channel_id=1, source_target_pairs={{0,4},{4,8},{8,12},{12,16},{16,20},{20,24},{24,28},{28,32},{32,36}... | collective-permute-start | bytes 36872 | tf_op jit(solution)/shard_map/ppermute | solution.py:23
  36.3 2.8 %collective-permute-start.5 = (f32[12,1,256]{2,1,0:T(1,128)S(1)}, f32[12,1,256]{2,1,0:T(1,128)S(1)}, u32[]{:S(2)}, u32[]{:S(2)}) collective-permute-start(f32[12,1,256]{2,1,0:T(1,128)S(1)} %get-tuple-element.63), channel_id=1, source_target_pairs={{4,0},{8,4},{12,8},{16,12},{20,16},{24,20},{28,24},{32,28},{36,32}... | collective-permute-start | bytes 36872 | tf_op jit(solution)/shard_map/ppermute | solution.py:25
  44.0 6.1 %collective-permute-start.7 = (f32[12,98,1]{1,2,0:T(1,128)}, f32[12,98,1]{1,2,0:T(1,128)}, u32[]{:S(2)}, u32[]{:S(2)}) collective-permute-start(f32[12,98,1]{1,2,0:T(1,128)} %copy.27), channel_id=1, source_target_pairs={{1,0},{2,1},{3,2},{0,3},{5,4},{6,5},{7,6},{4,7},{9,8},{10,9},{11,1... | collective-permute-start | bytes 14120 | tf_op jit(solution)/shard_map/ppermute | solution.py:25
  44.0 5.2 %collective-permute-start.6 = (f32[12,98,1]{1,2,0:T(1,128)}, f32[12,98,1]{1,2,0:T(1,128)}, u32[]{:S(2)}, u32[]{:S(2)}) collective-permute-start(f32[12,98,1]{1,2,0:T(1,128)} %copy.26), channel_id=1, source_target_pairs={{0,1},{1,2},{2,3},{3,0},{4,5},{5,6},{6,7},{7,4},{8,9},{9,10},{10,1... | collective-permute-start | bytes 14120 | tf_op jit(solution)/shard_map/ppermute | solution.py:23
  52.0 2.0 copy-start.35
  52.0 2.0 copy-start.39
  52.0 2.0 copy-start.43
  53.9 0.9 copy-start.9
  54.0 0.9 copy-start.19
  100.5 1.7 copy-start.58
  100.5 1.7 copy-start.13
  106.7 2.6 copy-start.6
  106.7 2.6 copy-start.16
  120.5 4.6 %copy-start.3 = (f32[12,96,256]{2,1,0:T(8,128)}, f32[12,96,256]{2,1,0:T(8,128)S(1)}, u32[]{:S(2)}) copy-start(f32[12,96,256]{2,1,0:T(8,128)S(1)} %fusion.34) | copy-start | bytes 3538948
  120.5 3.2 %collective-permute-start.8 = (f32[12,1,256]{2,1,0:T(1,128)S(1)}, f32[12,1,256]{2,1,0:T(1,128)S(1)}, u32[]{:S(2)}, u32[]{:S(2)}) collective-permute-start(f32[12,1,256]{2,1,0:T(1,128)S(1)} %get-tuple-element.60), channel_id=1, source_target_pairs={{0,4},{4,8},{8,12},{12,16},{16,20},{20,24},{24,28},{28,32},{32,36}... | collective-permute-start | bytes 36872 | tf_op jit(solution)/shard_map/ppermute | solution.py:23
  120.6 3.1 %collective-permute-start.9 = (f32[12,1,256]{2,1,0:T(1,128)S(1)}, f32[12,1,256]{2,1,0:T(1,128)S(1)}, u32[]{:S(2)}, u32[]{:S(2)}) collective-permute-start(f32[12,1,256]{2,1,0:T(1,128)S(1)} %get-tuple-element.61), channel_id=1, source_target_pairs={{4,0},{8,4},{12,8},{16,12},{20,16},{24,20},{28,24},{32,28},{36,32}... | collective-permute-start | bytes 36872 | tf_op jit(solution)/shard_map/ppermute | solution.py:25
  128.1 5.2 %collective-permute-start.10 = (f32[12,98,1]{1,2,0:T(1,128)}, f32[12,98,1]{1,2,0:T(1,128)}, u32[]{:S(2)}, u32[]{:S(2)}) collective-permute-start(f32[12,98,1]{1,2,0:T(1,128)} %copy.33), channel_id=1, source_target_pairs={{0,1},{1,2},{2,3},{3,0},{4,5},{5,6},{6,7},{7,4},{8,9},{9,10},{10,1... | collective-permute-start | bytes 14120 | tf_op jit(solution)/shard_map/ppermute | solution.py:23
  130.1 4.1 %collective-permute-start.11 = (f32[12,98,1]{1,2,0:T(1,128)}, f32[12,98,1]{1,2,0:T(1,128)}, u32[]{:S(2)}, u32[]{:S(2)}) collective-permute-start(f32[12,98,1]{1,2,0:T(1,128)} %copy.34), channel_id=1, source_target_pairs={{1,0},{2,1},{3,2},{0,3},{5,4},{6,5},{7,6},{4,7},{9,8},{10,9},{11,1... | collective-permute-start | bytes 14120 | tf_op jit(solution)/shard_map/ppermute | solution.py:25
  136.1 2.4 copy-start.36
  136.1 2.4 copy-start.40
  136.1 2.4 copy-start.44
  138.5 0.9 copy-start.10
  139.4 40.4 %copy-start.61 = (f32[12]{0:T(128)S(1)}, f32[12]{0:T(128)}, u32[]{:S(2)}) copy-start(f32[12]{0:T(128)} %copy-done.60) | copy-start | bytes 148
  139.4 40.4 %copy-start.63 = (f32[12]{0:T(128)S(1)}, f32[12]{0:T(128)}, u32[]{:S(2)}) copy-start(f32[12]{0:T(128)} %copy-done.62) | copy-start | bytes 148
  180.3 2.2 copy-start.50
  180.3 2.2 copy-start.52
  180.4 2.2 copy-start.14
  182.6 3.2 %copy-start = (f32[12,96,256]{2,1,0:T(8,128)}, f32[12,96,256]{2,1,0:T(8,128)S(1)}, u32[]{:S(2)}) copy-start(f32[12,96,256]{2,1,0:T(8,128)S(1)} %get-tuple-element.36) | copy-start | bytes 3538948
  187.1 2.6 copy-start.7
  187.1 2.6 copy-start.17
  201.3 3.6 %copy-start.2 = (f32[12,96,256]{2,1,0:T(8,128)}, f32[12,96,256]{2,1,0:T(8,128)S(1)}, u32[]{:S(2)}) copy-start(f32[12,96,256]{2,1,0:T(8,128)S(1)} %fusion.32) | copy-start | bytes 3538948
  201.3 3.4 %collective-permute-start.12 = (f32[12,1,256]{2,1,0:T(1,128)S(1)}, f32[12,1,256]{2,1,0:T(1,128)S(1)}, u32[]{:S(2)}, u32[]{:S(2)}) collective-permute-start(f32[12,1,256]{2,1,0:T(1,128)S(1)} %get-tuple-element.58), channel_id=1, source_target_pairs={{0,4},{4,8},{8,12},{12,16},{16,20},{20,24},{24,28},{28,32},{32,36}... | collective-permute-start | bytes 36872 | tf_op jit(solution)/shard_map/ppermute | solution.py:23
  201.6 3.1 %collective-permute-start.13 = (f32[12,1,256]{2,1,0:T(1,128)S(1)}, f32[12,1,256]{2,1,0:T(1,128)S(1)}, u32[]{:S(2)}, u32[]{:S(2)}) collective-permute-start(f32[12,1,256]{2,1,0:T(1,128)S(1)} %get-tuple-element.59), channel_id=1, source_target_pairs={{4,0},{8,4},{12,8},{16,12},{20,16},{24,20},{28,24},{32,28},{36,32}... | collective-permute-start | bytes 36872 | tf_op jit(solution)/shard_map/ppermute | solution.py:25
  207.3 4.9 %collective-permute-start.14 = (f32[12,98,1]{1,2,0:T(1,128)S(1)}, f32[12,98,1]{1,2,0:T(1,128)S(1)}, u32[]{:S(2)}, u32[]{:S(2)}) collective-permute-start(f32[12,98,1]{1,2,0:T(1,128)S(1)} %copy.40), channel_id=1, source_target_pairs={{0,1},{1,2},{2,3},{3,0},{4,5},{5,6},{6,7},{7,4},{8,9},{9,10},{10,1... | collective-permute-start | bytes 14120 | tf_op jit(solution)/shard_map/ppermute | solution.py:23
  207.6 4.9 %collective-permute-start.15 = (f32[12,98,1]{1,2,0:T(1,128)S(1)}, f32[12,98,1]{1,2,0:T(1,128)S(1)}, u32[]{:S(2)}, u32[]{:S(2)}) collective-permute-start(f32[12,98,1]{1,2,0:T(1,128)S(1)} %copy.41), channel_id=1, source_target_pairs={{1,0},{2,1},{3,2},{0,3},{5,4},{6,5},{7,6},{4,7},{9,8},{10,9},{11,1... | collective-permute-start | bytes 14120 | tf_op jit(solution)/shard_map/ppermute | solution.py:25
  213.6 2.3 copy-start.37
  213.6 2.3 copy-start.41
  213.6 2.4 copy-start.45
  216.0 1.3 copy-start.1
  216.0 1.3 copy-start.21
  216.0 1.3 copy-start.29
  216.0 1.2 copy-start.33
  216.0 1.2 copy-start.49
  217.3 41.3 %copy-start.56 = (f32[12]{0:T(128)S(1)}, f32[12]{0:T(128)}, u32[]{:S(2)}) copy-start(f32[12]{0:T(128)} %copy-done.55) | copy-start | bytes 148
  217.3 41.3 %copy-start.57 = (f32[12]{0:T(128)S(1)}, f32[12]{0:T(128)}, u32[]{:S(2)}) copy-start(f32[12]{0:T(128)} %get-tuple-element.38) | copy-start | bytes 148
  217.3 41.3 %copy-start.51 = (f32[12]{0:T(128)S(1)}, f32[12]{0:T(128)}, u32[]{:S(2)}) copy-start(f32[12]{0:T(128)} %copy-done.50) | copy-start | bytes 148
  217.3 41.3 %copy-start.53 = (f32[12]{0:T(128)S(1)}, f32[12]{0:T(128)}, u32[]{:S(2)}) copy-start(f32[12]{0:T(128)} %copy-done.52) | copy-start | bytes 148
  217.3 41.3 %copy-start.59 = (f32[12]{0:T(128)S(1)}, f32[12]{0:T(128)}, u32[]{:S(2)}) copy-start(f32[12]{0:T(128)} %copy-done.58) | copy-start | bytes 148
  (16 other events, 11.8 us)
where the time goes:
time: 269 us; the launch traced here: 264 us
  blocking collectives  121 us (45%)
  local copies, waits for them, and re-layouts  39.5 us (15%)
  other arithmetic  38.9 us (14%)
  matrix products  29.8 us (11%)
  starting transfers between devices  19.4 us (7%)
  waiting for transfers between devices  13.2 us (5%)
    psum x12, blocking collectives, one_axis_at_a_time(): return functools.reduce(lax.psum, axes, x)  121 us
    dot_general x7, matrix products, along_rows(): jnp.einsum('ka,mxkc->mxac', table, shaped, precision=lax.Precision.HIGHEST)  19 us
    ppermute x8, starting transfers between devices, extended(): lax.ppermute(head, axis, [((i + 1) % count, i) for i in range(count)])  14.8 us
    ppermute x8, waiting for transfers between devices, extended(): lax.ppermute(tail, axis, [(i, (i + 1) % count) for i in range(count)])  12.9 us
    slice x11, local copies, waits for them, and re-layouts, extended(): lax.slice_in_dim(cells, cells.shape[dim] - width, cells.shape[dim], axis=...  11.2 us
    dot_general x7, matrix products, along_cols(): result = jnp.matmul(shaped, table, precision=lax.Precision.HIGHEST)  10.8 us
    concatenate x8, other arithmetic, extended(): jnp.concatenate([lax.ppermute(tail, axis, [(i, (i + 1) % count) for i in...  8.18 us
    reshape x3, local copies, waits for them, and re-layouts, along_rows(): return result.reshape(mode_count, row_count, col_count)  6.69 us
  transfers between devices with their start and end apart: 16, of which 9 were waited for; matrix products, arithmetic and copies ran while one was open for 2% of the time, Pallas kernels for 0%

commit v1 on v0

v1 whole, which is shorter than its diff:
```python
import functools
import math

import jax
import jax.numpy as jnp
import numpy as np
from jax import lax
from jax.experimental import pallas as pl
from jax.experimental.pallas import tpu as pltpu
from jax.sharding import PartitionSpec as P

MESH = pl.DeviceIdType.MESH
EDGES = ((0, 1), (0, 2), (0, 3), (1, 2), (1, 3), (2, 3))
F32 = jnp.float32


def gll_slopes():
    points = np.array([-1.0, -1.0 / math.sqrt(5.0), 1.0 / math.sqrt(5.0), 1.0])
    factor = np.array(
        [np.prod([points[j] - points[m] for m in range(4) if m != j]) for j in range(4)]
    )
    slopes = np.zeros((4, 4))
    for i in range(4):
        for j in range(4):
            if i != j:
                slopes[i, j] = factor[i] / (factor[j] * (points[i] - points[j]))
        slopes[i, i] = sum((1.0 / (points[i] - points[m]) for m in range(4) if m != i))
    return slopes


def kernel(
    cfg,
    scale_ref,
    f_hbm,
    met_hbm,
    jac_hbm,
    x_ref,
    r_ref,
    fbuf,
    metbuf,
    jacbuf,
    w0,
    w1,
    w2,
    w3,
    y0,
    y1,
    y2,
    minv,
    mass,
    cx,
    cy,
    dots,
    rowbuf,
    colbuf,
    rowrecv,
    cornrecv,
    colrecv,
    rowfix,
    colfix,
    red,
    in_sems,
    send_sems,
    recv_sems,
    rs_send,
    rs_recv,
):
    n_modes, n_curve, n_sub, n_zc = cfg
    n_y = n_curve // n_zc
    c = lax.axis_index("curve")
    s = lax.axis_index("sub")
    c_prev, c_next = lax.rem(c + n_curve - 1, n_curve), lax.rem(c + 1, n_curve)
    s_prev, s_next = lax.rem(s + n_sub - 1, n_sub), lax.rem(s + 1, n_sub)
    y_pos, zc_pos = c // n_zc, lax.rem(c, n_zc)
    b_size = n_y * n_sub
    b_pos = y_pos * n_sub + s

    halves = (pl.ds(0, 128), pl.ds(128, 128))
    loads = []
    for h in range(2):
        loads.append(pltpu.make_async_copy(met_hbm.at[:, halves[h]], metbuf.at[h], in_sems.at[0, h]))
        loads.append(pltpu.make_async_copy(jac_hbm.at[:, halves[h]], jacbuf.at[h], in_sems.at[1, h]))
    for m in range(n_modes):
        for h in range(2):
            loads.append(
                pltpu.make_async_copy(f_hbm.at[m, :, halves[h]], fbuf.at[m, h], in_sems.at[2 + m, h])
            )
    for load in loads:
        load.start()

    def a_member(d):
        pos = lax.rem(zc_pos + d, n_zc)
        return (y_pos * n_zc + pos, s)

    def b_member(d):
        pos = lax.rem(b_pos + d, b_size)
        return ((pos // n_sub) * n_zc + zc_pos, lax.rem(pos, n_sub))

    around = [
        (c_prev, s), (c_next, s), (c, s_prev), (c, s_next),
        (c_prev, s_prev), (c_prev, s_next), (c_next, s_prev), (c_next, s_next),
    ]
    partners = around + [a_member(d) for d in range(1, n_zc)] + [b_member(d) for d in range(1, b_size)]
    barrier = pltpu.get_barrier_semaphore()
    for device in partners:
        pl.semaphore_signal(barrier, inc=1, device_id=device, device_id_type=MESH)

    lane = lax.broadcasted_iota(jnp.int32, (8, 128), 1)
    subl = lax.broadcasted_iota(jnp.int32, (8, 128), 0)
    phase = lane & 3
    lane24 = lax.broadcasted_iota(jnp.int32, (24, 128), 1)
    row24 = lax.broadcasted_iota(jnp.int32, (24, 256), 0)
    slopes = gll_slopes()

    def by_phase(values):
        out = jnp.full((8, 128), F32(values[3]))
        for b in (2, 1, 0):
            out = jnp.where(phase == b, F32(values[b]), out)
        return out

    def block(t):
        return pl.multiple_of((t // 2) * 8, 8), pl.multiple_of(lax.rem(t, 2) * 128, 128)

    def natural(r0, a):
        return pl.ds(a + 4 * r0, 8, stride=4)

    weights = (1.0 / 6.0, 5.0 / 6.0, 5.0 / 6.0, 1.0 / 6.0)
    col_w = by_phase(weights)
    col_count = by_phase((0.5, 1.0, 1.0, 0.5))

    def coupling(d, shift):
        vals = []
        for b in range(4):
            ok = 0 <= b + shift < 4 and b + d < 4
            vals.append(slopes[b + shift, b] * slopes[b + shift, b + d] if ok else 0.0)
        return by_phase(vals)

    for load in loads[:4]:
        load.wait()
    shifts = range(-3, 4)
    pair_tab = {(d, q): coupling(d, q) for d in (0, 1, 2, 3) for q in shifts}

    def setup(t, carry):
        r0, l0 = block(t)
        rows, cols = pl.ds(r0, 8), pl.ds(l0, 128)
        flux = []
        for a in range(4):
            grid_w = col_w * F32(weights[a])
            m_a = jacbuf[l0 // 128, natural(r0, a), :] * grid_w
            mass[a, rows, cols] = m_a
            w0[n_modes, a, rows, cols] = m_a
            flux.append(metbuf[l0 // 128, natural(r0, a), :] * grid_w)
        for e, (i, j) in enumerate(EDGES):
            total = flux[0] * F32(slopes[0, i] * slopes[0, j])
            for q in range(1, 4):
                total = total + flux[q] * F32(slopes[q, i] * slopes[q, j])
            cx[e, rows, cols] = total
        for a in range(4):
            rolled = {q: flux[a] if q == 0 else pltpu.roll(flux[a], (-q) % 128, 1) for q in shifts}
            lap = flux[0] * F32(slopes[0, a] ** 2)
            for q in range(1, 4):
                lap = lap + flux[q] * F32(slopes[q, a] ** 2)
            for q in shifts:
                lap = lap + rolled[q] * pair_tab[0, q]
            w0[n_modes + 1, a, rows, cols] = lap
            for d in (1, 2, 3):
                total = None
                for q in range(-3, 4):
                    if not any(0 <= b + q < 4 and b + d < 4 for b in range(4)):
                        continue
                    term = rolled[q] * pair_tab[d, q]
                    total = term if total is None else total + term
                cy[d - 1, a, rows, cols] = total
        return carry

    lax.fori_loop(0, 6, setup, 0)
    for load in loads[4:]:
        load.wait()

    def weigh(t, carry):
        r0, l0 = block(t)
        rows, cols = pl.ds(r0, 8), pl.ds(l0, 128)
        for a in range(4):
            m_a = mass[a, rows, cols]
            for m in range(n_modes):
                w0[m, a, rows, cols] = fbuf[m, l0 // 128, natural(r0, a), :] * m_a
        return carry

    lax.fori_loop(0, 6, weigh, 0)
    dots[...] = jnp.zeros_like(dots)

    def row_join_and_pack(e, w, count):
        packed = jnp.zeros((24, 128), F32)
        for m in range(count):
            top, bottom = w[m, 0], w[m, 3]
            bottom = bottom + jnp.where(row24 < 23, pltpu.roll(top, 23, 0), 0.0)
            top = jnp.where(row24 > 0, pltpu.roll(bottom, 1, 0), top)
            w[m, 0] = top
            w[m, 3] = bottom
            rowbuf[e, 0, m : m + 1, :] = top[0:1, :]
            rowbuf[e, 1, m : m + 1, :] = bottom[23:24, :]
            for a, plane in enumerate((top, w[m, 1], w[m, 2], bottom)):
                k = 4 * m + a
                ends = jnp.where(lane24 == 127, plane[:, 128:], plane[:, :128])
                ends = pltpu.roll(ends, 2 * k, 1) if k else ends
                packed = jnp.where(
                    (lane24 == 2 * k) | (lane24 == (2 * k - 1) % 128), ends, packed
                )
        colbuf[e] = packed

    def copies(e):
        low, high = pl.ds(0, 128), pl.ds(128, 128)
        plan = [
            (rowbuf.at[e, 1], rowrecv.at[e, 0], (c_next, s)),
            (rowbuf.at[e, 0], rowrecv.at[e, 1], (c_prev, s)),
            (colbuf.at[e], colrecv.at[e, 0], (c, s_next)),
            (colbuf.at[e], colrecv.at[e, 1], (c, s_prev)),
            (rowbuf.at[e, 1, :, high], cornrecv.at[e, 0], (c_next, s_next)),
            (rowbuf.at[e, 1, :, low], cornrecv.at[e, 1], (c_next, s_prev)),
            (rowbuf.at[e, 0, :, high], cornrecv.at[e, 2], (c_prev, s_next)),
            (rowbuf.at[e, 0, :, low], cornrecv.at[e, 3], (c_prev, s_prev)),
        ]
        return [
            pltpu.make_async_remote_copy(
                src_ref=src,
                dst_ref=dst,
                send_sem=send_sems.at[e, i],
                recv_sem=recv_sems.at[e, i],
                device_id=device,
                device_id_type=MESH,
            )
            for i, (src, dst, device) in enumerate(plan)
        ]

    def col_join(plane):
        lanes = lax.broadcasted_iota(jnp.int32, (plane.shape[0], 128), 1)
        last, first = lanes == 127, lanes == 0
        high_end, low_end = (lanes & 3) == 3, (lanes & 3) == 0
        x0, x1 = plane[:, :128], plane[:, 128:]
        n0, n1 = pltpu.roll(x0, 127, 1), pltpu.roll(x1, 127, 1)
        s0 = x0 + jnp.where(last, n1, n0)
        s1 = x1 + jnp.where(last, 0.0, n1)
        p0, p1 = pltpu.roll(s0, 1, 1), pltpu.roll(s1, 1, 1)
        out0 = jnp.where(high_end, s0, jnp.where(low_end, jnp.where(first, x0, p0), x0))
        out1 = jnp.where(high_end, s1, jnp.where(low_end, jnp.where(first, p0, p1), x1))
        return out0, out1

    def exchange(e, w, count):
        row_join_and_pack(e, w, count)
        if e == 0:
            pl.semaphore_wait(barrier, len(partners))
        sent = copies(e)
        for copy in sent:
            copy.start()
        for m in range(count):
            for a in range(4):
                out0, out1 = col_join(w[m, a])
                w[m, a, :, 0:128] = out0
                w[m, a, :, 128:256] = out1
        return sent

    def arrive(e, sent):
        for copy in sent:
            copy.wait_recv()
        lanes = lax.broadcasted_iota(jnp.int32, (16, 128), 1)
        for side in range(2):
            out0, out1 = col_join(rowrecv[e, side])
            left = pltpu.roll(cornrecv[e, 2 * side], 1, 1)
            right = pltpu.roll(cornrecv[e, 2 * side + 1], 127, 1)
            rowfix[side, :, 0:128] = out0 + jnp.where(lanes == 0, left, 0.0)
            rowfix[side, :, 128:256] = out1 + jnp.where(lanes == 127, right, 0.0)
        colfix[...] = jnp.where(
            (lane24 & 1) == 0, pltpu.roll(colrecv[e, 0], 1, 1), pltpu.roll(colrecv[e, 1], 127, 1)
        )

    def fixed(w, m, a, r0, l0):
        rows, cols = pl.ds(r0, 8), pl.ds(l0, 128)
        k = 4 * m + a
        ends = colfix[rows, :]
        ends = pltpu.roll(ends, (-2 * k) % 128, 1) if k else ends
        at = lane + l0
        value = w[m, a, rows, cols] + jnp.where((at == 0) | (at == 255), ends, 0.0)
        if a == 0:
            value = value + jnp.where(subl + r0 == 0, rowfix[0, m : m + 1, cols], 0.0)
        if a == 3:
            value = value + jnp.where(subl + r0 == 23, rowfix[1, m : m + 1, cols], 0.0)
        return value

    def total4(values):
        return (values[0] + values[1]) + (values[2] + values[3])

    def step(k, w_in, w_out, y_old, y_new, t):
        r0, l0 = block(t)
        rows, cols = pl.ds(r0, 8), pl.ds(l0, 128)
        if k == 0:
            mass_diag = [fixed(w_in, n_modes, a, r0, l0) for a in range(4)]
            lap_diag = [fixed(w_in, n_modes + 1, a, r0, l0) for a in range(4)]
        cxs = [cx[e, rows, cols] for e in range(6)]
        for m in range(n_modes):
            scale = scale_ref[m]
            vec, rhs, old = [], [], []
            for a in range(4):
                value = fixed(w_in, m, a, r0, l0)
                w_in[m, a, rows, cols] = value
                rhs.append(value)
                if k == 0:
                    inv = 1.0 / (mass_diag[a] + scale * lap_diag[a])
                    minv[m, a, rows, cols] = inv
                    vec.append(value * inv)
                else:
                    old.append(y_old[m, a, rows, cols])
                    vec.append(value * minv[m, a, rows, cols] - old[a])
                y_new[m, a, rows, cols] = vec[a]
            lap = [None] * 4
            for e, (i, j) in enumerate(EDGES):
                flow = cxs[e] * (vec[j] - vec[i])
                lap[i] = flow if lap[i] is None else lap[i] + flow
                lap[j] = -flow if lap[j] is None else lap[j] - flow
            image = []
            for a in range(4):
                v, total = vec[a], lap[a]
                for d in (1, 2, 3):
                    flow = cy[d - 1, a, rows, cols] * (pltpu.roll(v, 128 - d, 1) - v)
                    total = total + flow - pltpu.roll(flow, d, 1)
                h = mass[a, rows, cols] * v + scale * total
                w_out[m, a, rows, cols] = h
                image.append(h)
            if k == 0:
                prod = [u * v for u, v in zip(vec, rhs)]
                part = (0.5 * (prod[0] + prod[3]) + (prod[1] + prod[2])) * col_count
                dots[0, m] += part
                dots[1, m] += total4([u * v for u, v in zip(vec, image)])
            else:
                dots[2 * k, m] += total4([u * v for u, v in zip(old, image)])
                dots[2 * k + 1, m] += total4([u * v for u, v in zip(vec, image)])

    def run_step(*args):
        def body(t, carry):
            step(*args, t)
            return carry

        lax.fori_loop(0, 6, body, 0)

    sent0 = exchange(0, w0, n_modes + 2)
    arrive(0, sent0)
    run_step(0, w0, w1, None, y0)
    sent1 = exchange(1, w1, n_modes)
    arrive(1, sent1)
    run_step(1, w1, w2, y0, y1)
    sent2 = exchange(2, w2, n_modes)
    arrive(2, sent2)
    run_step(2, w2, w3, y1, y2)

    local = jnp.zeros((8, 128), F32)
    for m in range(n_modes):
        stacked = jnp.zeros((8, 128), F32)
        for q in range(6):
            stacked = jnp.where(subl == q, jnp.sum(dots[q, m], axis=0, keepdims=True), stacked)
        local = jnp.where(lane == m, jnp.sum(stacked, axis=1, keepdims=True), local)

    def phase_sum(p, value, size, pos, member):
        red[p, pos] = value
        moves = [
            pltpu.make_async_remote_copy(
                src_ref=red.at[p, pos],
                dst_ref=red.at[p, pos],
                send_sem=rs_send.at[p, d - 1],
                recv_sem=rs_recv.at[p, d - 1],
                device_id=member(d),
                device_id_type=MESH,
            )
            for d in range(1, size)
        ]
        for move in moves:
            move.start()
        return moves

    def phase_end(p, size, moves):
        for move in moves:
            move.wait_recv()
        parts = [red[p, i] for i in range(size)]
        while len(parts) > 1:
            parts = [
                parts[i] + parts[i + 1] if i + 1 < len(parts) else parts[i]
                for i in range(0, len(parts), 2)
            ]
        return parts[0]

    moves_a = phase_sum(0, local, n_zc, zc_pos, a_member)
    sent3 = exchange(3, w3, n_modes)
    moves_b = phase_sum(1, phase_end(0, n_zc, moves_a), b_size, b_pos, b_member)
    arrive(3, sent3)
    g = phase_end(1, b_size, moves_b)

    b0, k00, k01, k11, k12, k22 = (g[q : q + 1, :] for q in range(6))
    k02 = k11
    b1 = k00 - b0
    b2 = k01 - b1
    l10 = k01 / k00
    l20 = k02 / k00
    d1 = k11 - l10 * k01
    e12 = k12 - l10 * k02
    l21 = e12 / d1
    d2 = k22 - l20 * k02 - l21 * e12
    c1 = b1 - l10 * b0
    c2 = b2 - l20 * b0 - l21 * c1
    a2 = c2 / d2
    a1 = c1 / d1 - l21 * a2
    a0 = b0 / k00 - l10 * a1 - l20 * a2
    coef = [
        [jnp.broadcast_to(v[:, m : m + 1], (8, 128)) for v in (a0, a1, a2)] for m in range(n_modes)
    ]

    def finish(t, carry):
        r0, l0 = block(t)
        rows, cols = pl.ds(r0, 8), pl.ds(l0, 128)
        for m in range(n_modes):
            u0, u1, u2 = coef[m]
            for a in range(4):
                x_ref[m, l0 // 128, natural(r0, a), :] = (
                    u0 * y0[m, a, rows, cols] + u1 * y1[m, a, rows, cols] + u2 * y2[m, a, rows, cols]
                )
                r_ref[m, l0 // 128, natural(r0, a), :] = (
                    w0[m, a, rows, cols]
                    - u0 * w1[m, a, rows, cols]
                    - u1 * w2[m, a, rows, cols]
                    - u2 * fixed(w3, m, a, r0, l0)
                )
        return carry

    lax.fori_loop(0, 6, finish, 0)
    for group in (sent0, sent1, sent2, sent3, moves_a, moves_b):
        for copy in group:
            copy.wait_send()


def solution(mesh, n_zc=None):
    n_curve, n_sub = mesh.shape["curve"], mesh.shape["sub"]
    n_zc = n_zc or 16
    n_y = n_curve // n_zc

    def step(forcing, metric, jacobian, mode_scale):
        n_modes, n_rows, n_cols = forcing.shape
        vec = pltpu.VMEM((n_modes, 4, 24, 256), F32)
        dma = pltpu.SemaphoreType.DMA
        cfg = (n_modes, n_curve, n_sub, n_zc)
        out = jax.ShapeDtypeStruct((n_modes, 2, n_rows, 128), F32)
        outs = pl.pallas_call(
            functools.partial(kernel, cfg),
            out_shape=(out, out),
            in_specs=[pl.BlockSpec(memory_space=pltpu.SMEM)]
            + [pl.BlockSpec(memory_space=pltpu.HBM)] * 3,
            out_specs=(pl.BlockSpec(memory_space=pltpu.VMEM),) * 2,
            scratch_shapes=[
                pltpu.VMEM((n_modes, 2, n_rows, 128), F32),
                pltpu.VMEM((2, n_rows, 128), F32),
                pltpu.VMEM((2, n_rows, 128), F32),
                pltpu.VMEM((n_modes + 2, 4, 24, 256), F32),
                vec, vec, vec, vec, vec, vec, vec,
                pltpu.VMEM((4, 24, 256), F32),
                pltpu.VMEM((6, 24, 256), F32),
                pltpu.VMEM((3, 4, 24, 256), F32),
                pltpu.VMEM((6, n_modes, 8, 128), F32),
                pltpu.VMEM((4, 2, 16, 256), F32),
                pltpu.VMEM((4, 24, 128), F32),
                pltpu.VMEM((4, 2, 16, 256), F32),
                pltpu.VMEM((4, 4, 16, 128), F32),
                pltpu.VMEM((4, 2, 24, 128), F32),
                pltpu.VMEM((2, 16, 256), F32),
                pltpu.VMEM((24, 128), F32),
                pltpu.VMEM((2, max(n_zc, n_y * n_sub), 8, 128), F32),
                dma((2 + n_modes, 2)),
                dma((4, 8)),
                dma((4, 8)),
                dma((2, max(n_zc, n_y * n_sub))),
                dma((2, max(n_zc, n_y * n_sub))),
            ],
            compiler_params=pltpu.CompilerParams(
                collective_id=0, has_side_effects=True, vmem_limit_bytes=40 * 1024 * 1024
            ),
        )(mode_scale, forcing, metric, jacobian)
        return tuple(jnp.swapaxes(o, 1, 2).reshape(forcing.shape) for o in outs)

    return jax.shard_map(
        step,
        mesh=mesh,
        in_specs=(P(None, "curve", "sub"), P("curve", "sub"), P("curve", "sub"), P()),
        out_specs=(P(None, "curve", "sub"), P(None, "curve", "sub")),
        check_vma=False,
    )
```

time: 269 us -> 65.2 us (0.24)
  the two profiles are of different devices: /device:TPU:40 before, /device:TPU:1 now
where the time goes in v1:
time: 65.2 us; the launch traced here: 65 us
  Pallas kernels  59 us (90%)
  local copies, waits for them, and re-layouts  5.31 us (8%)
    pallas_call x1, Pallas kernels, step(): pl.pallas_call(functools.partial(kernel, cfg), out_shape=(out, out), in_s...  59 us
    unnamed x8, local copies, waits for them, and re-layouts  3.7 us
    reshape x1, local copies, waits for them, and re-layouts, step(): return tuple((jnp.swapaxes(o, 1, 2).reshape(forcing.shape) for o in outs))  1.61 us

profile of v1, /device:TPU:1, one launch (start us, length us, event | category | flops | bytes accessed | tf_op | source)
XLA Modules:
  0.0 65.0 jit_solution(16318079973762164045)
XLA Ops:
  0.6 0.0 copy-start
  0.6 1.3 %copy-done = f32[12,96,256]{2,1,0:T(8,128)S(1)} copy-done((f32[12,96,256]{2,1,0:T(8,128)S(1)}, f32[12,96,256]{2,1,0:T(8,128)}, u32[]{:S(2)}) %copy-start) | copy-done | bytes 1179672
  1.9 0.0 copy-start.1
  1.9 0.9 %copy-done.1 = f32[96,256]{1,0:T(8,128)S(1)} copy-done((f32[96,256]{1,0:T(8,128)S(1)}, f32[96,256]{1,0:T(8,128)}, u32[]{:S(2)}) %copy-start.1) | copy-done | bytes 98328
  2.8 0.0 copy-start.2
  2.8 0.9 %copy-done.2 = f32[96,256]{1,0:T(8,128)S(1)} copy-done((f32[96,256]{1,0:T(8,128)S(1)}, f32[96,256]{1,0:T(8,128)}, u32[]{:S(2)}) %copy-start.2) | copy-done | bytes 98328
  3.7 0.0 copy-start.3
  3.7 0.7 %copy-done.3 = f32[12]{0:T(128)S(1)} copy-done((f32[12]{0:T(128)S(1)}, f32[12]{0:T(128)}, u32[]{:S(2)}) %copy-start.3) | copy-done | bytes 72
  4.3 59.0 %shard_map.59 = (f32[12,2,96,128]{3,2,1,0:T(8,128)S(1)}, f32[12,2,96,128]{3,2,1,0:T(8,128)S(1)}) custom-call(f32[12]{0:T(128)S(1)} %copy-done.3, f32[12,96,256]{2,1,0:T(8,128)S(1)} %copy-done, f32[96,256]{1,0:T(8,128)S(1)} %copy-done.1, f32[96,256]{1,0:T(8,128)S(1)} %copy-done.2), custom_call_target="tpu_custom_call" | custom-call | tf_op jit(solution)/shard_map/pallas_call | solution.py:448
  63.4 1.6 %copy_bitcast_fusion = (f32[12,96,256]{2,1,0:T(8,128)}, f32[12,96,256]{2,1,0:T(8,128)}) fusion(f32[12,2,96,128]{3,2,1,0:T(8,128)S(1)} %get-tuple-element.4, f32[12,2,96,128]{3,2,1,0:T(8,128)S(1)} %get-tuple-element.5), kind=kLoop, calls=%fused_computation | loop fusion | bytes 4718592 | tf_op jit(solution)/shard_map/reshape | solution.py:482
Async XLA Ops:
  0.6 1.3 %copy-start = (f32[12,96,256]{2,1,0:T(8,128)S(1)}, f32[12,96,256]{2,1,0:T(8,128)}, u32[]{:S(2)}) copy-start(f32[12,96,256]{2,1,0:T(8,128)} %f_hbm.1) | copy-start | bytes 3538948
  1.9 0.9 %copy-start.1 = (f32[96,256]{1,0:T(8,128)S(1)}, f32[96,256]{1,0:T(8,128)}, u32[]{:S(2)}) copy-start(f32[96,256]{1,0:T(8,128)} %met_hbm.1) | copy-start | bytes 294916
  2.8 0.9 %copy-start.2 = (f32[96,256]{1,0:T(8,128)S(1)}, f32[96,256]{1,0:T(8,128)}, u32[]{:S(2)}) copy-start(f32[96,256]{1,0:T(8,128)} %jac_hbm.1) | copy-start | bytes 294916
  3.7 0.7 %copy-start.3 = (f32[12]{0:T(128)S(1)}, f32[12]{0:T(128)}, u32[]{:S(2)}) copy-start(f32[12]{0:T(128)} %scale_ref.1) | copy-start | bytes 148

commit v2 on v1

v2 whole, which is shorter than its diff:
```python
import functools
import math

import jax
import jax.numpy as jnp
import numpy as np
from jax import lax
from jax.experimental import pallas as pl
from jax.experimental.pallas import tpu as pltpu
from jax.sharding import PartitionSpec as P

MESH = pl.DeviceIdType.MESH
EDGES = ((0, 1), (0, 2), (0, 3), (1, 2), (1, 3), (2, 3))
F32 = jnp.float32
VMEM_LIMIT = 61 * 1024 * 1024


def gll_slopes():
    points = np.array([-1.0, -1.0 / math.sqrt(5.0), 1.0 / math.sqrt(5.0), 1.0])
    factor = np.array(
        [np.prod([points[j] - points[m] for m in range(4) if m != j]) for j in range(4)]
    )
    slopes = np.zeros((4, 4))
    for i in range(4):
        for j in range(4):
            if i != j:
                slopes[i, j] = factor[i] / (factor[j] * (points[i] - points[j]))
        slopes[i, i] = sum((1.0 / (points[i] - points[m]) for m in range(4) if m != i))
    return slopes


def kernel(
    cfg,
    scale_ref,
    f_hbm,
    met_hbm,
    jac_hbm,
    x_ref,
    r_ref,
    fbuf,
    metbuf,
    jacbuf,
    w0,
    w1,
    w2,
    w3,
    y0,
    y1,
    y2,
    minv,
    nat,
    mass,
    cx,
    cy,
    perm,
    dots,
    rowbuf,
    cornbuf,
    colbuf,
    rowrecv,
    cornrecv,
    colrecv,
    rowfix,
    colfix,
    red,
    in_sems,
    send_sems,
    recv_sems,
    rs_send,
    rs_recv,
):
    n_modes, n_curve, n_sub, n_zc = cfg
    n_pairs = n_modes // 2
    n_y = n_curve // n_zc
    c = lax.axis_index("curve")
    s = lax.axis_index("sub")
    c_prev, c_next = lax.rem(c + n_curve - 1, n_curve), lax.rem(c + 1, n_curve)
    s_prev, s_next = lax.rem(s + n_sub - 1, n_sub), lax.rem(s + 1, n_sub)
    y_pos, zc_pos = c // n_zc, lax.rem(c, n_zc)
    b_size = n_y * n_sub
    b_pos = y_pos * n_sub + s

    halves = (pl.ds(0, 128), pl.ds(128, 128))
    loads = []
    for h in range(2):
        loads.append(pltpu.make_async_copy(met_hbm.at[:, halves[h]], metbuf.at[h], in_sems.at[0, h]))
        loads.append(pltpu.make_async_copy(jac_hbm.at[:, halves[h]], jacbuf.at[h], in_sems.at[1, h]))
    for m in range(n_modes):
        for h in range(2):
            loads.append(
                pltpu.make_async_copy(f_hbm.at[m, :, halves[h]], fbuf.at[m, h], in_sems.at[2 + m, h])
            )
    for load in loads:
        load.start()

    def a_member(d):
        pos = lax.rem(zc_pos + d, n_zc)
        return (y_pos * n_zc + pos, s)

    def b_member(d):
        pos = lax.rem(b_pos + d, b_size)
        return ((pos // n_sub) * n_zc + zc_pos, lax.rem(pos, n_sub))

    around = [
        (c_prev, s), (c_next, s), (c, s_prev), (c, s_next),
        (c_prev, s_prev), (c_prev, s_next), (c_next, s_prev), (c_next, s_next),
    ]
    partners = around + [a_member(d) for d in range(1, n_zc)] + [b_member(d) for d in range(1, b_size)]
    barrier = pltpu.get_barrier_semaphore()
    for device in partners:
        pl.semaphore_signal(barrier, inc=1, device_id=device, device_id_type=MESH)

    def lanes_of(rows):
        return lax.broadcasted_iota(jnp.int32, (rows, 128), 1)

    def rows_of(rows):
        return lax.broadcasted_iota(jnp.int32, (rows, 128), 0)

    lane, subl = lanes_of(8), rows_of(8)
    at_low, at_high, low_half = (lane & 63) == 0, (lane & 63) == 63, lane < 64
    slopes = gll_slopes()
    weights = (1.0 / 6.0, 5.0 / 6.0, 5.0 / 6.0, 1.0 / 6.0)

    big_r = lax.broadcasted_iota(jnp.int32, (256, 256), 0)
    big_c = lax.broadcasted_iota(jnp.int32, (256, 256), 1)
    for odd in range(2):
        into = ((big_r & 3) ^ odd) * 64 + (big_r >> 2) == big_c
        back = ((big_c & 3) ^ odd) * 64 + (big_c >> 2) == big_r
        perm[odd] = jnp.where(into, 1.0, 0.0).astype(jnp.bfloat16)
        perm[2 + odd] = jnp.where(back, 1.0, 0.0).astype(jnp.bfloat16)

    def select_exact(x, which):
        high = x.astype(jnp.bfloat16)
        rest = x - high.astype(F32)
        mid = rest.astype(jnp.bfloat16)
        low = (rest - mid.astype(F32)).astype(jnp.bfloat16)
        matrix = perm[which]

        def dot(part):
            return jnp.dot(part, matrix, preferred_element_type=F32)

        return (dot(high) + dot(mid)) + dot(low)

    def natural(buf):
        return jnp.concatenate(
            [
                jnp.concatenate([buf[h, pl.ds(a, 24, stride=4), :] for a in range(4)], axis=0)
                for h in range(2)
            ],
            axis=1,
        )

    def deinterleave(x_even, x_odd):
        lo = lanes_of(96) < 64
        even, odd = select_exact(x_even, 0), select_exact(x_odd, 1)
        out = []
        for q in range(2):
            e, o = even[:, 128 * q : 128 * (q + 1)], odd[:, 128 * q : 128 * (q + 1)]
            out.append(jnp.where(lo, e, o))
            out.append(pltpu.roll(jnp.where(lo, o, e), 64, 1))
        return out

    def to_natural(slot, planes, p):
        lo = lanes_of(96) < 64
        full = [jnp.concatenate([planes[p, a, b] for a in range(4)], axis=0) for b in range(4)]
        odd1, odd3 = pltpu.roll(full[1], 64, 1), pltpu.roll(full[3], 64, 1)
        even = jnp.concatenate([jnp.where(lo, full[0], odd1), jnp.where(lo, full[2], odd3)], axis=1)
        odd = jnp.concatenate([jnp.where(lo, odd1, full[0]), jnp.where(lo, odd3, full[2])], axis=1)
        for par, packed in enumerate((even, odd)):
            out = select_exact(packed, 2 + par)
            for h in range(2):
                nat[slot, 2 * p + par, h] = out[:, 128 * h : 128 * (h + 1)]

    for load in loads[:4]:
        load.wait()
    for target, buf in ((mass, jacbuf), (minv, metbuf)):
        x = natural(buf)
        for b, plane in enumerate(deinterleave(x, x)):
            for a in range(4):
                grid_w = F32(weights[a]) * F32(weights[b])
                value = plane[24 * a : 24 * (a + 1)] * grid_w
                if target is mass:
                    mass[a, b] = value
                else:
                    minv[0, a, b] = value

    def setup(t, carry):
        rows = pl.ds(pl.multiple_of(t * 8, 8), 8)
        flux = [[minv[0, a, b, rows, :] for b in range(4)] for a in range(4)]

        def mix(values, table):
            total = values[0] * F32(table[0])
            for q in range(1, 4):
                total = total + values[q] * F32(table[q])
            return total

        for b in range(4):
            column = [flux[q][b] for q in range(4)]
            for e, (i, j) in enumerate(EDGES):
                table = slopes[:, i] * slopes[:, j]
                cx[e, b, rows, :] = mix(column, table)
                cy[e, b, rows, :] = mix(flux[b], table)
            for a in range(4):
                lap = mix(column, slopes[:, a] ** 2) + mix(flux[a], slopes[:, b] ** 2)
                w0[n_pairs, a, b, rows, :] = jnp.where(low_half, mass[a, b, rows, :], lap)
        return carry

    lax.fori_loop(0, 3, setup, 0)
    dots[...] = jnp.zeros_like(dots)
    rowbuf[...] = jnp.zeros_like(rowbuf)
    cornbuf[...] = jnp.zeros_like(cornbuf)

    for p in range(n_pairs):
        for load in loads[4 + 4 * p : 8 + 4 * p]:
            load.wait()
        planes = deinterleave(natural(fbuf.at[2 * p]), natural(fbuf.at[2 * p + 1]))
        for b in range(4):
            for a in range(4):
                w0[p, a, b] = planes[b][24 * a : 24 * (a + 1)] * mass[a, b]

    lane24, row24 = lanes_of(24), rows_of(24)
    pack_key = ((lane24 + 1) & 63) >> 1

    def row_join_and_pack(e, w, pairs):
        packed = jnp.zeros((24, 128), F32)
        for p in range(pairs):
            ends = [None] * 4
            tops, bottoms = [], []
            for b in range(4):
                top, bottom = w[p, 0, b], w[p, 3, b]
                bottom = bottom + jnp.where(row24 < 23, pltpu.roll(top, 23, 0), 0.0)
                top = jnp.where(row24 > 0, pltpu.roll(bottom, 1, 0), top)
                w[p, 0, b] = top
                w[p, 3, b] = bottom
                r = 4 * p + b
                rowbuf[e, 0, r : r + 1, :] = top[0:1, :]
                rowbuf[e, 1, r : r + 1, :] = bottom[23:24, :]
                tops.append(top)
                bottoms.append(bottom)
            low_end = lane24 & 63 == 0
            corner_end = low_end[0:1]
            cornbuf[e, 0, p : p + 1, :] = jnp.where(corner_end, tops[0][0:1], tops[3][0:1])
            cornbuf[e, 1, p : p + 1, :] = jnp.where(corner_end, bottoms[0][23:24], bottoms[3][23:24])
            first = (tops[0], w[p, 1, 0], w[p, 2, 0], bottoms[0])
            last = (tops[3], w[p, 1, 3], w[p, 2, 3], bottoms[3])
            for a in range(4):
                k = 4 * p + a
                ends = jnp.where(low_end, first[a], last[a])
                ends = pltpu.roll(ends, 2 * k, 1) if k else ends
                packed = jnp.where(pack_key == k, ends, packed)
        colbuf[e] = packed

    def copies(e, pairs):
        part = pl.ds(0, -(-4 * pairs // 8) * 8)
        plan = [
            (rowbuf.at[e, 1, part], rowrecv.at[e, 0, part], (c_next, s)),
            (rowbuf.at[e, 0, part], rowrecv.at[e, 1, part], (c_prev, s)),
            (colbuf.at[e], colrecv.at[e, 0], (c, s_next)),
            (colbuf.at[e], colrecv.at[e, 1], (c, s_prev)),
            (cornbuf.at[e, 1], cornrecv.at[e, 0], (c_next, s_next)),
            (cornbuf.at[e, 1], cornrecv.at[e, 1], (c_next, s_prev)),
            (cornbuf.at[e, 0], cornrecv.at[e, 2], (c_prev, s_next)),
            (cornbuf.at[e, 0], cornrecv.at[e, 3], (c_prev, s_prev)),
        ]
        return [
            pltpu.make_async_remote_copy(
                src_ref=src,
                dst_ref=dst,
                send_sem=send_sems.at[e, i],
                recv_sem=recv_sems.at[e, i],
                device_id=device,
                device_id_type=MESH,
            )
            for i, (src, dst, device) in reversed(list(enumerate(plan)))
        ]

    def exchange(e, w, pairs):
        row_join_and_pack(e, w, pairs)
        if e == 0:
            pl.semaphore_wait(barrier, len(partners))
        sent = copies(e, pairs)
        for copy in sent:
            copy.start()
        inner_high, inner_low = lane24 & 63 != 63, lane24 & 63 != 0
        for p in range(pairs):
            for a in range(4):
                first, last = w[p, a, 0], w[p, a, 3]
                last = last + jnp.where(inner_high, pltpu.roll(first, 127, 1), 0.0)
                w[p, a, 3] = last
                w[p, a, 0] = jnp.where(inner_low, pltpu.roll(last, 1, 1), first)
        return sent

    def arrive(e, sent, pairs):
        for copy in sent:
            copy.wait_recv()
        count = -(-4 * pairs // 8) * 8
        lanes, rows = lanes_of(count) & 63, rows_of(count) & 3
        for side in range(2):
            r = rowrecv[e, side, 0:count, :]
            t = pltpu.roll(pltpu.roll(r, 127, 1), 3, 0)
            u = r + jnp.where((rows == 3) & (lanes != 63), t, 0.0)
            v = pltpu.roll(pltpu.roll(u, 1, 1), count - 3, 0)
            rowfix[side, 0:count, :] = jnp.where((rows == 0) & (lanes != 0), v, u)
            left = pltpu.roll(cornrecv[e, 2 * side], 65, 1)
            right = pltpu.roll(cornrecv[e, 2 * side + 1], 63, 1)
            left = jnp.where(at_low, left, 0.0)
            right = jnp.where(at_high, right, 0.0)
            for p in range(pairs):
                rowfix[side, 4 * p : 4 * p + 1, :] += left[p : p + 1]
                rowfix[side, 4 * p + 3 : 4 * p + 4, :] += right[p : p + 1]
        colfix[...] = jnp.where(
            (lane24 & 1) == 0, pltpu.roll(colrecv[e, 0], 65, 1), pltpu.roll(colrecv[e, 1], 63, 1)
        )

    def fixed(w, p, r0):
        rows = pl.ds(r0, 8)
        out = []
        for a in range(4):
            k = 4 * p + a
            ends = colfix[rows, :]
            ends = pltpu.roll(ends, (-2 * k) % 128, 1) if k else ends
            line = []
            for b in range(4):
                value = w[p, a, b, rows, :]
                if b == 0:
                    value = value + jnp.where(at_low, ends, 0.0)
                if b == 3:
                    value = value + jnp.where(at_high, ends, 0.0)
                r = 4 * p + b
                if a == 0:
                    value = value + jnp.where(subl + r0 == 0, rowfix[0, r : r + 1, :], 0.0)
                if a == 3:
                    value = value + jnp.where(subl + r0 == 23, rowfix[1, r : r + 1, :], 0.0)
                line.append(value)
            out.append(line)
        return out

    def total(values):
        values = list(values)
        while len(values) > 1:
            values = [
                values[i] + values[i + 1] if i + 1 < len(values) else values[i]
                for i in range(0, len(values), 2)
            ]
        return values[0]

    quad = [(a, b) for a in range(4) for b in range(4)]

    def step(k, w_in, w_out, y_old, y_new, t):
        r0 = pl.multiple_of(t * 8, 8)
        rows = pl.ds(r0, 8)
        if k == 0:
            both = fixed(w_in, n_pairs, r0)
            for a, b in quad:
                swapped = pltpu.roll(both[a][b], 64, 1)
                w_in[n_pairs, a, b, rows, :] = jnp.where(low_half, both[a][b], swapped)
                y2[0, a, b, rows, :] = jnp.where(low_half, swapped, both[a][b])
        for p in range(n_pairs):
            scale = jnp.where(low_half, scale_ref[2 * p], scale_ref[2 * p + 1])
            value = fixed(w_in, p, r0)
            vec = [[None] * 4 for _ in range(4)]
            for a, b in quad:
                w_in[p, a, b, rows, :] = value[a][b]
                if k == 0:
                    diag = w_in[n_pairs, a, b, rows, :] + scale * y2[0, a, b, rows, :]
                    inv = 1.0 / diag
                    minv[p, a, b, rows, :] = inv
                    vec[a][b] = value[a][b] * inv
                else:
                    vec[a][b] = value[a][b] * minv[p, a, b, rows, :] - y_old[p, a, b, rows, :]
                y_new[p, a, b, rows, :] = vec[a][b]
            lap = [[None] * 4 for _ in range(4)]

            def flow(table, e, line, i, j):
                (ai, bi), (aj, bj) = i, j
                f = table[e, line, rows, :] * (vec[aj][bj] - vec[ai][bi])
                lap[ai][bi] = f if lap[ai][bi] is None else lap[ai][bi] + f
                lap[aj][bj] = -f if lap[aj][bj] is None else lap[aj][bj] - f

            for line in range(4):
                for e, (i, j) in enumerate(EDGES):
                    flow(cx, e, line, (i, line), (j, line))
            image = [[None] * 4 for _ in range(4)]
            for a in range(4):
                for e, (i, j) in enumerate(EDGES):
                    flow(cy, e, a, (a, i), (a, j))
                for b in range(4):
                    image[a][b] = mass[a, b, rows, :] * vec[a][b] + scale * lap[a][b]
                    w_out[p, a, b, rows, :] = image[a][b]
            if k == 0:
                count = (0.5, 1.0, 1.0, 0.5)
                terms = []
                for a, b in quad:
                    term = vec[a][b] * value[a][b]
                    weight = count[a] * count[b]
                    terms.append(term if weight == 1.0 else term * F32(weight))
                dots[0, p] += total(terms)
                dots[1, p] += total(vec[a][b] * image[a][b] for a, b in quad)
            else:
                dots[2 * k, p] += total(y_old[p, a, b, rows, :] * image[a][b] for a, b in quad)
                dots[2 * k + 1, p] += total(vec[a][b] * image[a][b] for a, b in quad)

    def run_step(*args):
        def body(t, carry):
            step(*args, t)
            return carry

        lax.fori_loop(0, 3, body, 0)

    sent0 = exchange(0, w0, n_pairs + 1)
    arrive(0, sent0, n_pairs + 1)
    run_step(0, w0, w1, None, y0)
    sent1 = exchange(1, w1, n_pairs)
    arrive(1, sent1, n_pairs)
    run_step(1, w1, w2, y0, y1)
    sent2 = exchange(2, w2, n_pairs)
    arrive(2, sent2, n_pairs)
    run_step(2, w2, w3, y1, y2)

    local = jnp.zeros((8, 128), F32)
    for p in range(n_pairs):
        stacked = jnp.zeros((8, 128), F32)
        for q in range(6):
            stacked = jnp.where(subl == q, jnp.sum(dots[q, p], axis=0, keepdims=True), stacked)
        for par in range(2):
            half = jnp.where(low_half, stacked, 0.0) if par == 0 else jnp.where(low_half, 0.0, stacked)
            local = jnp.where(lane == 2 * p + par, jnp.sum(half, axis=1, keepdims=True), local)

    def phase_start(i, value, size, pos, member):
        red[i, pos] = value
        moves = [
            pltpu.make_async_remote_copy(
                src_ref=red.at[i, pos],
                dst_ref=red.at[i, pos],
                send_sem=rs_send.at[i, d - 1],
                recv_sem=rs_recv.at[i, d - 1],
                device_id=member(d),
                device_id_type=MESH,
            )
            for d in range(1, size)
        ]
        for move in moves:
            move.start()
        return moves

    def phase_end(i, size, moves):
        for move in moves:
            move.wait_recv()
        return total(red[i, j] for j in range(size))

    def run_natural(slot, planes):
        for p in range(n_pairs):
            to_natural(slot, planes, p)

    moves_a = phase_start(0, local, n_zc, zc_pos, a_member)
    sent3 = exchange(3, w3, n_pairs)
    for slot, planes in enumerate((y0, y1, y2)):
        run_natural(slot, planes)
    moves_b = phase_start(1, phase_end(0, n_zc, moves_a), b_size, b_pos, b_member)
    for slot, planes in enumerate((w0, w1, w2)):
        run_natural(3 + slot, planes)
    arrive(3, sent3, n_pairs)

    def last_fix(t, carry):
        r0 = pl.multiple_of(t * 8, 8)
        for p in range(n_pairs):
            value = fixed(w3, p, r0)
            for a, b in quad:
                w3[p, a, b, pl.ds(r0, 8), :] = value[a][b]
        return carry

    lax.fori_loop(0, 3, last_fix, 0)
    run_natural(6, w3)
    g = phase_end(1, b_size, moves_b)

    b0, k00, k01, k11, k12, k22 = (g[q : q + 1, :] for q in range(6))
    k02 = k11
    b1 = k00 - b0
    b2 = k01 - b1
    l10 = k01 / k00
    l20 = k02 / k00
    d1 = k11 - l10 * k01
    e12 = k12 - l10 * k02
    l21 = e12 / d1
    d2 = k22 - l20 * k02 - l21 * e12
    c1 = b1 - l10 * b0
    c2 = b2 - l20 * b0 - l21 * c1
    a2 = c2 / d2
    a1 = c1 / d1 - l21 * a2
    a0 = b0 / k00 - l10 * a1 - l20 * a2

    for m in range(n_modes):
        u0, u1, u2 = (jnp.broadcast_to(v[:, m : m + 1], (8, 128)) for v in (a0, a1, a2))
        for h in range(2):
            for a in range(4):
                for t in range(3):
                    src = pl.ds(24 * a + 8 * t, 8)
                    dst = pl.ds(a + 32 * t, 8, stride=4)
                    n = [nat[i, m, h, src, :] for i in range(7)]
                    x_ref[m, h, dst, :] = u0 * n[0] + u1 * n[1] + u2 * n[2]
                    r_ref[m, h, dst, :] = n[3] - u0 * n[4] - u1 * n[5] - u2 * n[6]
    for group in (sent0, sent1, sent2, sent3, moves_a, moves_b):
        for copy in group:
            copy.wait_send()


def solution(mesh, n_zc=None):
    n_curve, n_sub = mesh.shape["curve"], mesh.shape["sub"]
    n_zc = n_zc or 16
    n_y = n_curve // n_zc

    def step(forcing, metric, jacobian, mode_scale):
        n_modes, n_rows, n_cols = forcing.shape
        n_pairs = n_modes // 2
        vec = pltpu.VMEM((n_pairs, 4, 4, 24, 128), F32)
        dma = pltpu.SemaphoreType.DMA
        cfg = (n_modes, n_curve, n_sub, n_zc)
        out = jax.ShapeDtypeStruct((n_modes, 2, n_rows, 128), F32)
        slots = max(n_zc, n_y * n_sub)
        outs = pl.pallas_call(
            functools.partial(kernel, cfg),
            out_shape=(out, out),
            in_specs=[pl.BlockSpec(memory_space=pltpu.SMEM)]
            + [pl.BlockSpec(memory_space=pltpu.HBM)] * 3,
            out_specs=(pl.BlockSpec(memory_space=pltpu.VMEM),) * 2,
            scratch_shapes=[
                pltpu.VMEM((n_modes, 2, n_rows, 128), F32),
                pltpu.VMEM((2, n_rows, 128), F32),
                pltpu.VMEM((2, n_rows, 128), F32),
                pltpu.VMEM((n_pairs + 1, 4, 4, 24, 128), F32),
                vec, vec, vec, vec, vec, vec, vec,
                pltpu.VMEM((7, n_modes, 2, n_rows, 128), F32),
                pltpu.VMEM((4, 4, 24, 128), F32),
                pltpu.VMEM((6, 4, 24, 128), F32),
                pltpu.VMEM((6, 4, 24, 128), F32),
                pltpu.VMEM((4, 256, 256), jnp.bfloat16),
                pltpu.VMEM((6, n_pairs, 8, 128), F32),
                pltpu.VMEM((4, 2, 32, 128), F32),
                pltpu.VMEM((4, 2, 8, 128), F32),
                pltpu.VMEM((4, 24, 128), F32),
                pltpu.VMEM((4, 2, 32, 128), F32),
                pltpu.VMEM((4, 4, 8, 128), F32),
                pltpu.VMEM((4, 2, 24, 128), F32),
                pltpu.VMEM((2, 32, 128), F32),
                pltpu.VMEM((24, 128), F32),
                pltpu.VMEM((2, slots, 8, 128), F32),
                dma((2 + n_modes, 2)),
                dma((4, 8)),
                dma((4, 8)),
                dma((2, slots)),
                dma((2, slots)),
            ],
            compiler_params=pltpu.CompilerParams(
                collective_id=0, has_side_effects=True, vmem_limit_bytes=VMEM_LIMIT
            ),
        )(mode_scale, forcing, metric, jacobian)
        return tuple(jnp.swapaxes(o, 1, 2).reshape(forcing.shape) for o in outs)

    return jax.shard_map(
        step,
        mesh=mesh,
        in_specs=(P(None, "curve", "sub"), P("curve", "sub"), P("curve", "sub"), P()),
        out_specs=(P(None, "curve", "sub"), P(None, "curve", "sub")),
        check_vma=False,
    )
```

time: 65.2 us -> 45.2 us (0.69)
  Pallas kernels: 59 us -> 41.1 us
  local copies, waits for them, and re-layouts: 5.31 us -> 3.24 us
    pallas_call x1, Pallas kernels: 59 us -> 41.1 us  [step(): pl.pallas_call(functools.partial(kernel, cfg), out_shape=(out, out), in_s...]
    unnamed x8 -> x0, local copies, waits for them, and re-layouts: 3.7 us -> none
    reshape x1, local copies, waits for them, and re-layouts: 1.61 us -> 3.24 us  [step(): return tuple((jnp.swapaxes(o, 1, 2).reshape(forcing.shape) for o in outs))]
where the time goes in v2:
time: 45.2 us; the launch traced here: 45 us
  Pallas kernels  41.1 us (91%)
  local copies, waits for them, and re-layouts  3.24 us (7%)
  between operations  0.64 us (1%)
    pallas_call x1, Pallas kernels, step(): pl.pallas_call(functools.partial(kernel, cfg), out_shape=(out, out), in_s...  41.1 us
    reshape x1, local copies, waits for them, and re-layouts, step(): return tuple((jnp.swapaxes(o, 1, 2).reshape(forcing.shape) for o in outs))  3.24 us

profile of v2, /device:TPU:1, one launch (start us, length us, event | category | flops | bytes accessed | tf_op | source)
XLA Modules:
  0.0 45.0 jit_solution(12454864257045518147)
XLA Ops:
  0.6 41.1 %shard_map.59 = (f32[12,2,96,128]{3,2,1,0:T(8,128)}, f32[12,2,96,128]{3,2,1,0:T(8,128)}) custom-call(f32[12]{0:T(128)} %scale_ref.1, f32[12,96,256]{2,1,0:T(8,128)} %f_hbm.1, f32[96,256]{1,0:T(8,128)} %met_hbm.1, f32[96,256]{1,0:T(8,128)} %jac_hbm.1), custom_call_target="tpu_custom_call" | custom-call | tf_op jit(solution)/shard_map/pallas_call | solution.py:520
  41.7 3.2 %copy_bitcast_fusion = (f32[12,96,256]{2,1,0:T(8,128)}, f32[12,96,256]{2,1,0:T(8,128)}) fusion(f32[12,2,96,128]{3,2,1,0:T(8,128)} %get-tuple-element.4, f32[12,2,96,128]{3,2,1,0:T(8,128)} %get-tuple-element.5), kind=kLoop, calls=%fused_computation | loop fusion | bytes 4718592 | tf_op jit(solution)/shard_map/reshape | solution.py:557

commit v3 on v2

--- a/solution.py
+++ b/solution.py
@@ -12,7 +12,7 @@
 MESH = pl.DeviceIdType.MESH
 EDGES = ((0, 1), (0, 2), (0, 3), (1, 2), (1, 3), (2, 3))
 F32 = jnp.float32
-VMEM_LIMIT = 61 * 1024 * 1024
+VMEM_LIMIT = 40 * 1024 * 1024
 
 
 def gll_slopes():
@@ -31,12 +31,13 @@
 
 def kernel(
     cfg,
-    scale_ref,
+    scale_hbm,
     f_hbm,
     met_hbm,
     jac_hbm,
     x_ref,
     r_ref,
+    scale_ref,
     fbuf,
     metbuf,
     jacbuf,
@@ -90,6 +91,7 @@
             loads.append(
                 pltpu.make_async_copy(f_hbm.at[m, :, halves[h]], fbuf.at[m, h], in_sems.at[2 + m, h])
             )
+    loads.append(pltpu.make_async_copy(scale_hbm, scale_ref, in_sems.at[2 + n_modes, 0]))
     for load in loads:
         load.start()
 
@@ -271,7 +273,7 @@
                 device_id=device,
                 device_id_type=MESH,
             )
-            for i, (src, dst, device) in reversed(list(enumerate(plan)))
+            for i, (src, dst, device) in enumerate(plan)
         ]
 
     def exchange(e, w, pairs):
@@ -279,7 +281,7 @@
         if e == 0:
             pl.semaphore_wait(barrier, len(partners))
         sent = copies(e, pairs)
-        for copy in sent:
+        for copy in reversed(sent):
             copy.start()
         inner_high, inner_low = lane24 & 63 != 63, lane24 & 63 != 0
         for p in range(pairs):
@@ -290,8 +292,15 @@
                 w[p, a, 0] = jnp.where(inner_low, pltpu.roll(last, 1, 1), first)
         return sent
 
-    def arrive(e, sent, pairs):
-        for copy in sent:
+    def arrive_cols(e, sent):
+        for copy in sent[2:4]:
+            copy.wait_recv()
+        colfix[...] = jnp.where(
+            (lane24 & 1) == 0, pltpu.roll(colrecv[e, 0], 65, 1), pltpu.roll(colrecv[e, 1], 63, 1)
+        )
+
+    def arrive_rows(e, sent, pairs):
+        for copy in sent[:2] + sent[4:]:
             copy.wait_recv()
         count = -(-4 * pairs // 8) * 8
         lanes, rows = lanes_of(count) & 63, rows_of(count) & 3
@@ -308,11 +317,8 @@
             for p in range(pairs):
                 rowfix[side, 4 * p : 4 * p + 1, :] += left[p : p + 1]
                 rowfix[side, 4 * p + 3 : 4 * p + 4, :] += right[p : p + 1]
-        colfix[...] = jnp.where(
-            (lane24 & 1) == 0, pltpu.roll(colrecv[e, 0], 65, 1), pltpu.roll(colrecv[e, 1], 63, 1)
-        )
-
-    def fixed(w, p, r0):
+
+    def fixed(w, p, r0, outer):
         rows = pl.ds(r0, 8)
         out = []
         for a in range(4):
@@ -327,9 +333,9 @@
                 if b == 3:
                     value = value + jnp.where(at_high, ends, 0.0)
                 r = 4 * p + b
-                if a == 0:
+                if outer and a == 0:
                     value = value + jnp.where(subl + r0 == 0, rowfix[0, r : r + 1, :], 0.0)
-                if a == 3:
+                if outer and a == 3:
                     value = value + jnp.where(subl + r0 == 23, rowfix[1, r : r + 1, :], 0.0)
                 line.append(value)
             out.append(line)
@@ -346,18 +352,18 @@
 
     quad = [(a, b) for a in range(4) for b in range(4)]
 
-    def step(k, w_in, w_out, y_old, y_new, t):
-        r0 = pl.multiple_of(t * 8, 8)
+    def step(k, w_in, w_out, y_old, y_new, t, outer):
+        r0 = pl.multiple_of(t * 8, 8) if outer else 8 * t
         rows = pl.ds(r0, 8)
         if k == 0:
-            both = fixed(w_in, n_pairs, r0)
+            both = fixed(w_in, n_pairs, r0, outer)
             for a, b in quad:
                 swapped = pltpu.roll(both[a][b], 64, 1)
                 w_in[n_pairs, a, b, rows, :] = jnp.where(low_half, both[a][b], swapped)
                 y2[0, a, b, rows, :] = jnp.where(low_half, swapped, both[a][b])
         for p in range(n_pairs):
             scale = jnp.where(low_half, scale_ref[2 * p], scale_ref[2 * p + 1])
-            value = fixed(w_in, p, r0)
+            value = fixed(w_in, p, r0, outer)
             vec = [[None] * 4 for _ in range(4)]
             for a, b in quad:
                 w_in[p, a, b, rows, :] = value[a][b]
@@ -400,22 +406,23 @@
                 dots[2 * k, p] += total(y_old[p, a, b, rows, :] * image[a][b] for a, b in quad)
                 dots[2 * k + 1, p] += total(vec[a][b] * image[a][b] for a, b in quad)
 
-    def run_step(*args):
-        def body(t, carry):
-            step(*args, t)
+    def run_step(e, sent, pairs, *args):
+        def body(i, carry):
+            step(*args, 2 * i, True)
             return carry
 
-        lax.fori_loop(0, 3, body, 0)
+        arrive_cols(e, sent)
+        step(*args, 1, False)
+        arrive_rows(e, sent, pairs)
+        lax.fori_loop(0, 2, body, 0)
 
     sent0 = exchange(0, w0, n_pairs + 1)
-    arrive(0, sent0, n_pairs + 1)
-    run_step(0, w0, w1, None, y0)
+    loads[-1].wait()
+    run_step(0, sent0, n_pairs + 1, 0, w0, w1, None, y0)
     sent1 = exchange(1, w1, n_pairs)
-    arrive(1, sent1, n_pairs)
-    run_step(1, w1, w2, y0, y1)
+    run_step(1, sent1, n_pairs, 1, w1, w2, y0, y1)
     sent2 = exchange(2, w2, n_pairs)
-    arrive(2, sent2, n_pairs)
-    run_step(2, w2, w3, y1, y2)
+    run_step(2, sent2, n_pairs, 2, w2, w3, y1, y2)
 
     local = jnp.zeros((8, 128), F32)
     for p in range(n_pairs):
@@ -459,12 +466,13 @@
     moves_b = phase_start(1, phase_end(0, n_zc, moves_a), b_size, b_pos, b_member)
     for slot, planes in enumerate((w0, w1, w2)):
         run_natural(3 + slot, planes)
-    arrive(3, sent3, n_pairs)
+    arrive_cols(3, sent3)
+    arrive_rows(3, sent3, n_pairs)
 
     def last_fix(t, carry):
         r0 = pl.multiple_of(t * 8, 8)
         for p in range(n_pairs):
-            value = fixed(w3, p, r0)
+            value = fixed(w3, p, r0, True)
             for a, b in quad:
                 w3[p, a, b, pl.ds(r0, 8), :] = value[a][b]
         return carry
@@ -520,10 +528,10 @@
         outs = pl.pallas_call(
             functools.partial(kernel, cfg),
             out_shape=(out, out),
-            in_specs=[pl.BlockSpec(memory_space=pltpu.SMEM)]
-            + [pl.BlockSpec(memory_space=pltpu.HBM)] * 3,
+            in_specs=[pl.BlockSpec(memory_space=pltpu.HBM)] * 4,
             out_specs=(pl.BlockSpec(memory_space=pltpu.VMEM),) * 2,
             scratch_shapes=[
+                pltpu.SMEM((n_modes,), F32),
                 pltpu.VMEM((n_modes, 2, n_rows, 128), F32),
                 pltpu.VMEM((2, n_rows, 128), F32),
                 pltpu.VMEM((2, n_rows, 128), F32),
@@ -544,7 +552,7 @@
                 pltpu.VMEM((2, 32, 128), F32),
                 pltpu.VMEM((24, 128), F32),
                 pltpu.VMEM((2, slots, 8, 128), F32),
-                dma((2 + n_modes, 2)),
+                dma((3 + n_modes, 2)),
                 dma((4, 8)),
                 dma((4, 8)),
                 dma((2, slots)),
@@ -553,7 +561,12 @@
             compiler_params=pltpu.CompilerParams(
                 collective_id=0, has_side_effects=True, vmem_limit_bytes=VMEM_LIMIT
             ),
-        )(mode_scale, forcing, metric, jacobian)
+        )(
+            *(
+                pltpu.with_memory_space_constraint(v, pltpu.HBM)
+                for v in (mode_scale, forcing, metric, jacobian)
+            )
+        )
         return tuple(jnp.swapaxes(o, 1, 2).reshape(forcing.shape) for o in outs)
 
     return jax.shard_map(

time: 45.2 us -> 40.4 us (0.89)
  Pallas kernels: 41.1 us -> 38 us
  local copies, waits for them, and re-layouts: 3.24 us -> 1.61 us
    pallas_call x1, Pallas kernels: 41.1 us -> 38 us  [step(): pl.pallas_call(functools.partial(kernel, cfg), out_shape=(out, out), in_s...]
    reshape x1, local copies, waits for them, and re-layouts: 3.24 us -> 1.61 us  [step(): return tuple((jnp.swapaxes(o, 1, 2).reshape(forcing.shape) for o in outs))]
where the time goes in v3:
time: 40.4 us; the launch traced here: 40.2 us
  Pallas kernels  38 us (94%)
  local copies, waits for them, and re-layouts  1.61 us (4%)
  between operations  0.64 us (2%)
    pallas_call x1, Pallas kernels, step(): pl.pallas_call(functools.partial(kernel, cfg), out_shape=(out, out), in_s...  38 us
    reshape x1, local copies, waits for them, and re-layouts, step(): return tuple((jnp.swapaxes(o, 1, 2).reshape(forcing.shape) for o in outs))  1.61 us

profile of v3, /device:TPU:1, one launch (start us, length us, event | category | flops | bytes accessed | tf_op | source)
XLA Modules:
  0.0 40.2 jit_solution(7393088881189447735)
XLA Ops:
  0.6 38.0 %shard_map.59 = (f32[12,2,96,128]{3,2,1,0:T(8,128)S(1)}, f32[12,2,96,128]{3,2,1,0:T(8,128)S(1)}) custom-call(f32[12]{0:T(128)} %scale_hbm.1, f32[12,96,256]{2,1,0:T(8,128)} %f_hbm.1, f32[96,256]{1,0:T(8,128)} %met_hbm.1, f32[96,256]{1,0:T(8,128)} %jac_hbm.1), custom_call_target="tpu_custom_call" | custom-call | tf_op jit(solution)/shard_map/pallas_call | solution.py:528
  38.6 1.6 %copy_bitcast_fusion = (f32[12,96,256]{2,1,0:T(8,128)}, f32[12,96,256]{2,1,0:T(8,128)}) fusion(f32[12,2,96,128]{3,2,1,0:T(8,128)S(1)} %get-tuple-element.4, f32[12,2,96,128]{3,2,1,0:T(8,128)S(1)} %get-tuple-element.5), kind=kLoop, calls=%fused_computation | loop fusion | bytes 4718592 | tf_op jit(solution)/shard_map/reshape | solution.py:570

commit v4 on v3

--- a/solution.py
+++ b/solution.py
@@ -54,6 +54,7 @@
     cx,
     cy,
     perm,
+    edge,
     dots,
     rowbuf,
     cornbuf,
@@ -127,9 +128,7 @@
     big_c = lax.broadcasted_iota(jnp.int32, (256, 256), 1)
     for odd in range(2):
         into = ((big_r & 3) ^ odd) * 64 + (big_r >> 2) == big_c
-        back = ((big_c & 3) ^ odd) * 64 + (big_c >> 2) == big_r
         perm[odd] = jnp.where(into, 1.0, 0.0).astype(jnp.bfloat16)
-        perm[2 + odd] = jnp.where(back, 1.0, 0.0).astype(jnp.bfloat16)
 
     def select_exact(x, which):
         high = x.astype(jnp.bfloat16)
@@ -153,7 +152,7 @@
         )
 
     def deinterleave(x_even, x_odd):
-        lo = lanes_of(96) < 64
+        lo = lanes_of(x_even.shape[0]) < 64
         even, odd = select_exact(x_even, 0), select_exact(x_odd, 1)
         out = []
         for q in range(2):
@@ -212,51 +211,43 @@
     rowbuf[...] = jnp.zeros_like(rowbuf)
     cornbuf[...] = jnp.zeros_like(cornbuf)
 
-    for p in range(n_pairs):
-        for load in loads[4 + 4 * p : 8 + 4 * p]:
-            load.wait()
-        planes = deinterleave(natural(fbuf.at[2 * p]), natural(fbuf.at[2 * p + 1]))
+    lane24, row24 = lanes_of(24), rows_of(24)
+    low_end = (lane24 & 63) == 0
+    pack_key = ((lane24 + 1) & 63) >> 1
+    pack_key2 = ((lane24 + 1) & 127) >> 1
+
+    def row_join(w, p):
         for b in range(4):
-            for a in range(4):
-                w0[p, a, b] = planes[b][24 * a : 24 * (a + 1)] * mass[a, b]
-
-    lane24, row24 = lanes_of(24), rows_of(24)
-    pack_key = ((lane24 + 1) & 63) >> 1
-
-    def row_join_and_pack(e, w, pairs):
-        packed = jnp.zeros((24, 128), F32)
-        for p in range(pairs):
-            ends = [None] * 4
-            tops, bottoms = [], []
-            for b in range(4):
-                top, bottom = w[p, 0, b], w[p, 3, b]
-                bottom = bottom + jnp.where(row24 < 23, pltpu.roll(top, 23, 0), 0.0)
-                top = jnp.where(row24 > 0, pltpu.roll(bottom, 1, 0), top)
-                w[p, 0, b] = top
-                w[p, 3, b] = bottom
-                r = 4 * p + b
-                rowbuf[e, 0, r : r + 1, :] = top[0:1, :]
-                rowbuf[e, 1, r : r + 1, :] = bottom[23:24, :]
-                tops.append(top)
-                bottoms.append(bottom)
-            low_end = lane24 & 63 == 0
-            corner_end = low_end[0:1]
-            cornbuf[e, 0, p : p + 1, :] = jnp.where(corner_end, tops[0][0:1], tops[3][0:1])
-            cornbuf[e, 1, p : p + 1, :] = jnp.where(corner_end, bottoms[0][23:24], bottoms[3][23:24])
-            first = (tops[0], w[p, 1, 0], w[p, 2, 0], bottoms[0])
-            last = (tops[3], w[p, 1, 3], w[p, 2, 3], bottoms[3])
-            for a in range(4):
-                k = 4 * p + a
-                ends = jnp.where(low_end, first[a], last[a])
-                ends = pltpu.roll(ends, 2 * k, 1) if k else ends
-                packed = jnp.where(pack_key == k, ends, packed)
-        colbuf[e] = packed
-
-    def copies(e, pairs):
-        part = pl.ds(0, -(-4 * pairs // 8) * 8)
+            top, bottom = w[p, 0, b], w[p, 3, b]
+            w[p, 3, b] = bottom + jnp.where(row24 < 23, pltpu.roll(top, 23, 0), 0.0)
+            w[p, 0, b] = top + jnp.where(row24 > 0, pltpu.roll(bottom, 1, 0), 0.0)
+
+    def col_join(w, p):
+        inner_high, inner_low = lane24 & 63 != 63, lane24 & 63 != 0
+        for a in range(4):
+            first, last = w[p, a, 0], w[p, a, 3]
+            w[p, a, 3] = last + jnp.where(inner_high, pltpu.roll(first, 127, 1), 0.0)
+            w[p, a, 0] = first + jnp.where(inner_low, pltpu.roll(last, 1, 1), 0.0)
+
+    def pack_cols(w, p, packed):
+        for a in range(4):
+            k = 4 * p + a
+            ends = jnp.where(low_end, w[p, a, 0], w[p, a, 3])
+            ends = pltpu.roll(ends, 2 * k, 1) if k else ends
+            packed = jnp.where(pack_key == k, ends, packed)
+        return packed
+
+    def put_row(e, side, p, lines):
+        for b in range(4):
+            rowbuf[e, side, 8 * b + p : 8 * b + p + 1, :] = lines[b]
+
+    def put_corners(e, side):
+        cornbuf[e, side] = jnp.where(at_low, rowbuf[e, side, 0:8, :], rowbuf[e, side, 24:32, :])
+
+    def copies(e):
         plan = [
-            (rowbuf.at[e, 1, part], rowrecv.at[e, 0, part], (c_next, s)),
-            (rowbuf.at[e, 0, part], rowrecv.at[e, 1, part], (c_prev, s)),
+            (rowbuf.at[e, 1], rowrecv.at[e, 0], (c_next, s)),
+            (rowbuf.at[e, 0], rowrecv.at[e, 1], (c_prev, s)),
             (colbuf.at[e], colrecv.at[e, 0], (c, s_next)),
             (colbuf.at[e], colrecv.at[e, 1], (c, s_prev)),
             (cornbuf.at[e, 1], cornrecv.at[e, 0], (c_next, s_next)),
@@ -276,20 +267,81 @@
             for i, (src, dst, device) in enumerate(plan)
         ]
 
-    def exchange(e, w, pairs):
-        row_join_and_pack(e, w, pairs)
-        if e == 0:
-            pl.semaphore_wait(barrier, len(partners))
-        sent = copies(e, pairs)
-        for copy in reversed(sent):
+    def send_rows(sent, e, side):
+        put_corners(e, side)
+        for i in (6, 7, 1) if side == 0 else (4, 5, 0):
+            sent[i].start()
+
+    def send_cols(sent, e, w):
+        packed = jnp.zeros((24, 128), F32)
+        for p in range(n_pairs):
+            row_join(w, p)
+            packed = pack_cols(w, p, packed)
+        colbuf[e] = packed
+        for copy in sent[2:4]:
             copy.start()
-        inner_high, inner_low = lane24 & 63 != 63, lane24 & 63 != 0
-        for p in range(pairs):
-            for a in range(4):
-                first, last = w[p, a, 0], w[p, a, 3]
-                last = last + jnp.where(inner_high, pltpu.roll(first, 127, 1), 0.0)
-                w[p, a, 3] = last
-                w[p, a, 0] = jnp.where(inner_low, pltpu.roll(last, 1, 1), first)
+        for p in range(n_pairs):
+            col_join(w, p)
+
+    def first_exchange():
+        sent = copies(0)
+        edge[...] = jnp.zeros_like(edge)
+        for load in loads[4:-1]:
+            load.wait()
+        for m in range(n_modes):
+            for h in range(2):
+                for side in range(2):
+                    r, i = 8 * side + m // 2, 95 * side
+                    edge[m % 2, h, r : r + 1, :] = fbuf[m, h, i : i + 1, :]
+        planes = deinterleave(
+            *(jnp.concatenate([edge[par, 0], edge[par, 1]], axis=1) for par in range(2))
+        )
+        for side in range(2):
+            for b in range(4):
+                line = mass[0, b, 0:1, :] if side == 0 else mass[3, b, 23:24, :]
+                rowbuf[0, side, 8 * b : 8 * b + 8, :] = planes[b][8 * side : 8 * side + 8] * line
+        put_row(0, 0, n_pairs, [w0[n_pairs, 0, b, 0:1, :] for b in range(4)])
+        put_row(0, 1, n_pairs, [w0[n_pairs, 3, b, 23:24, :] for b in range(4)])
+        pl.semaphore_wait(barrier, len(partners))
+        send_rows(sent, 0, 0)
+        send_rows(sent, 0, 1)
+        packed = jnp.zeros((24, 128), F32)
+        for a in range(4):
+            every = pl.ds(a, 24, stride=4)
+            grid_w = F32(weights[a]) * F32(weights[0])
+            ends_mass = jnp.where(lane24 == 127, jacbuf[1, every, :], jacbuf[0, every, :]) * grid_w
+            for p in range(n_pairs):
+                for par in range(2):
+                    k = 4 * p + a + 32 * par
+                    ends = jnp.where(
+                        lane24 == 127, fbuf[2 * p + 1 - par, 1, every, :], fbuf[2 * p + par, 0, every, :]
+                    )
+                    ends = ends * ends_mass
+                    ends = pltpu.roll(ends, 2 * k, 1) if k else ends
+                    packed = jnp.where(pack_key2 == k, ends, packed)
+        below = pltpu.roll(pltpu.roll(packed, 6, 1), 23, 0)
+        above = pltpu.roll(pltpu.roll(packed, 122, 1), 1, 0)
+        packed = (
+            packed
+            + jnp.where(((pack_key & 3) == 3) & (row24 < 23), below, 0.0)
+            + jnp.where(((pack_key & 3) == 0) & (row24 > 0), above, 0.0)
+        )
+        row_join(w0, n_pairs)
+        colbuf[0] = pack_cols(w0, n_pairs, packed)
+        for copy in sent[2:4]:
+            copy.start()
+        for p in range(n_pairs):
+            planes = deinterleave(natural(fbuf.at[2 * p]), natural(fbuf.at[2 * p + 1]))
+            for b in range(4):
+                for a in range(4):
+                    w0[p, a, b] = planes[b][24 * a : 24 * (a + 1)] * mass[a, b]
+            row_join(w0, p)
+            col_join(w0, p)
+        col_join(w0, n_pairs)
+        for odd in range(2):
+            back = ((big_c & 3) ^ odd) * 64 + (big_c >> 2) == big_r
+            perm[2 + odd] = jnp.where(back, 1.0, 0.0).astype(jnp.bfloat16)
+        loads[-1].wait()
         return sent
 
     def arrive_cols(e, sent):
@@ -299,24 +351,17 @@
             (lane24 & 1) == 0, pltpu.roll(colrecv[e, 0], 65, 1), pltpu.roll(colrecv[e, 1], 63, 1)
         )
 
-    def arrive_rows(e, sent, pairs):
+    def arrive_rows(e, sent):
         for copy in sent[:2] + sent[4:]:
             copy.wait_recv()
-        count = -(-4 * pairs // 8) * 8
-        lanes, rows = lanes_of(count) & 63, rows_of(count) & 3
         for side in range(2):
-            r = rowrecv[e, side, 0:count, :]
-            t = pltpu.roll(pltpu.roll(r, 127, 1), 3, 0)
-            u = r + jnp.where((rows == 3) & (lanes != 63), t, 0.0)
-            v = pltpu.roll(pltpu.roll(u, 1, 1), count - 3, 0)
-            rowfix[side, 0:count, :] = jnp.where((rows == 0) & (lanes != 0), v, u)
+            r = [rowrecv[e, side, 8 * b : 8 * b + 8, :] for b in range(4)]
             left = pltpu.roll(cornrecv[e, 2 * side], 65, 1)
             right = pltpu.roll(cornrecv[e, 2 * side + 1], 63, 1)
-            left = jnp.where(at_low, left, 0.0)
-            right = jnp.where(at_high, right, 0.0)
-            for p in range(pairs):
-                rowfix[side, 4 * p : 4 * p + 1, :] += left[p : p + 1]
-                rowfix[side, 4 * p + 3 : 4 * p + 4, :] += right[p : p + 1]
+            rowfix[side, 0:8, :] = r[0] + jnp.where(at_low, left, pltpu.roll(r[3], 1, 1))
+            rowfix[side, 8:16, :] = r[1]
+            rowfix[side, 16:24, :] = r[2]
+            rowfix[side, 24:32, :] = r[3] + jnp.where(at_high, right, pltpu.roll(r[0], 127, 1))
 
     def fixed(w, p, r0, outer):
         rows = pl.ds(r0, 8)
@@ -332,7 +377,7 @@
                     value = value + jnp.where(at_low, ends, 0.0)
                 if b == 3:
                     value = value + jnp.where(at_high, ends, 0.0)
-                r = 4 * p + b
+                r = 8 * b + p
                 if outer and a == 0:
                     value = value + jnp.where(subl + r0 == 0, rowfix[0, r : r + 1, :], 0.0)
                 if outer and a == 3:
@@ -353,7 +398,7 @@
     quad = [(a, b) for a in range(4) for b in range(4)]
 
     def step(k, w_in, w_out, y_old, y_new, t, outer):
-        r0 = pl.multiple_of(t * 8, 8) if outer else 8 * t
+        r0 = 8 * t
         rows = pl.ds(r0, 8)
         if k == 0:
             both = fixed(w_in, n_pairs, r0, outer)
@@ -393,6 +438,9 @@
                 for b in range(4):
                     image[a][b] = mass[a, b, rows, :] * vec[a][b] + scale * lap[a][b]
                     w_out[p, a, b, rows, :] = image[a][b]
+            if outer:
+                side = t // 2
+                put_row(k + 1, side, p, [image[3 * side][b][7 * side : 7 * side + 1] for b in range(4)])
             if k == 0:
                 count = (0.5, 1.0, 1.0, 0.5)
                 terms = []
@@ -406,23 +454,22 @@
                 dots[2 * k, p] += total(y_old[p, a, b, rows, :] * image[a][b] for a, b in quad)
                 dots[2 * k + 1, p] += total(vec[a][b] * image[a][b] for a, b in quad)
 
-    def run_step(e, sent, pairs, *args):
-        def body(i, carry):
-            step(*args, 2 * i, True)
-            return carry
-
-        arrive_cols(e, sent)
-        step(*args, 1, False)
-        arrive_rows(e, sent, pairs)
-        lax.fori_loop(0, 2, body, 0)
-
-    sent0 = exchange(0, w0, n_pairs + 1)
-    loads[-1].wait()
-    run_step(0, sent0, n_pairs + 1, 0, w0, w1, None, y0)
-    sent1 = exchange(1, w1, n_pairs)
-    run_step(1, sent1, n_pairs, 1, w1, w2, y0, y1)
-    sent2 = exchange(2, w2, n_pairs)
-    run_step(2, sent2, n_pairs, 2, w2, w3, y1, y2)
+    def run_step(k, sent, w_in, w_out, y_old, y_new):
+        arrive_cols(k, sent)
+        step(k, w_in, w_out, y_old, y_new, 1, False)
+        arrive_rows(k, sent)
+        following = copies(k + 1)
+        for side in range(2):
+            step(k, w_in, w_out, y_old, y_new, 2 * side, True)
+            send_rows(following, k + 1, side)
+        return following
+
+    sent0 = first_exchange()
+    sent1 = run_step(0, sent0, w0, w1, None, y0)
+    send_cols(sent1, 1, w1)
+    sent2 = run_step(1, sent1, w1, w2, y0, y1)
+    send_cols(sent2, 2, w2)
+    sent3 = run_step(2, sent2, w2, w3, y1, y2)
 
     local = jnp.zeros((8, 128), F32)
     for p in range(n_pairs):
@@ -460,14 +507,14 @@
             to_natural(slot, planes, p)
 
     moves_a = phase_start(0, local, n_zc, zc_pos, a_member)
-    sent3 = exchange(3, w3, n_pairs)
+    send_cols(sent3, 3, w3)
     for slot, planes in enumerate((y0, y1, y2)):
         run_natural(slot, planes)
     moves_b = phase_start(1, phase_end(0, n_zc, moves_a), b_size, b_pos, b_member)
     for slot, planes in enumerate((w0, w1, w2)):
         run_natural(3 + slot, planes)
     arrive_cols(3, sent3)
-    arrive_rows(3, sent3, n_pairs)
+    arrive_rows(3, sent3)
 
     def last_fix(t, carry):
         r0 = pl.multiple_of(t * 8, 8)
@@ -542,6 +589,7 @@
                 pltpu.VMEM((6, 4, 24, 128), F32),
                 pltpu.VMEM((6, 4, 24, 128), F32),
                 pltpu.VMEM((4, 256, 256), jnp.bfloat16),
+                pltpu.VMEM((2, 2, 16, 128), F32),
                 pltpu.VMEM((6, n_pairs, 8, 128), F32),
                 pltpu.VMEM((4, 2, 32, 128), F32),
                 pltpu.VMEM((4, 2, 8, 128), F32),

time: 40.4 us -> 39.4 us (0.975)
  Pallas kernels: 38 us -> 37 us
    pallas_call x1, Pallas kernels: 38 us -> 37 us  [step(): pl.pallas_call(functools.partial(kernel, cfg), out_shape=(out, out), in_s...]
where the time goes in v4:
time: 39.4 us; the launch traced here: 39.3 us
  Pallas kernels  37 us (94%)
  local copies, waits for them, and re-layouts  1.61 us (4%)
  between operations  0.64 us (2%)
    pallas_call x1, Pallas kernels, step(): pl.pallas_call(functools.partial(kernel, cfg), out_shape=(out, out), in_s...  37 us
    reshape x1, local copies, waits for them, and re-layouts, step(): return tuple((jnp.swapaxes(o, 1, 2).reshape(forcing.shape) for o in outs))  1.61 us

profile of v4, /device:TPU:1, one launch (start us, length us, event | category | flops | bytes accessed | tf_op | source)
XLA Modules:
  0.0 39.3 jit_solution(15104445056628208250)
XLA Ops:
  0.6 37.0 %shard_map.59 = (f32[12,2,96,128]{3,2,1,0:T(8,128)S(1)}, f32[12,2,96,128]{3,2,1,0:T(8,128)S(1)}) custom-call(f32[12]{0:T(128)} %scale_hbm.1, f32[12,96,256]{2,1,0:T(8,128)} %f_hbm.1, f32[96,256]{1,0:T(8,128)} %met_hbm.1, f32[96,256]{1,0:T(8,128)} %jac_hbm.1), custom_call_target="tpu_custom_call" | custom-call | tf_op jit(solution)/shard_map/pallas_call | solution.py:575
  37.7 1.6 %copy_bitcast_fusion = (f32[12,96,256]{2,1,0:T(8,128)}, f32[12,96,256]{2,1,0:T(8,128)}) fusion(f32[12,2,96,128]{3,2,1,0:T(8,128)S(1)} %get-tuple-element.4, f32[12,2,96,128]{3,2,1,0:T(8,128)S(1)} %get-tuple-element.5), kind=kLoop, calls=%fused_computation | loop fusion | bytes 4718592 | tf_op jit(solution)/shard_map/reshape | solution.py:618

commit v5 on v4

--- a/solution.py
+++ b/solution.py
@@ -526,6 +526,9 @@
 
     lax.fori_loop(0, 3, last_fix, 0)
     run_natural(6, w3)
+    for group in (sent0, sent1, sent2, sent3, moves_a, moves_b):
+        for copy in group:
+            copy.wait_send()
     g = phase_end(1, b_size, moves_b)
 
     b0, k00, k01, k11, k12, k22 = (g[q : q + 1, :] for q in range(6))
@@ -554,9 +557,6 @@
                     n = [nat[i, m, h, src, :] for i in range(7)]
                     x_ref[m, h, dst, :] = u0 * n[0] + u1 * n[1] + u2 * n[2]
                     r_ref[m, h, dst, :] = n[3] - u0 * n[4] - u1 * n[5] - u2 * n[6]
-    for group in (sent0, sent1, sent2, sent3, moves_a, moves_b):
-        for copy in group:
-            copy.wait_send()
 
 
 def solution(mesh, n_zc=None):

time: 39.4 us -> 39.3 us (level)
  no operation moved by 1% of the time
where the time goes in v5:
time: 39.3 us; the launch traced here: 39.2 us
  Pallas kernels  36.9 us (94%)
  local copies, waits for them, and re-layouts  1.61 us (4%)
  between operations  0.64 us (2%)
    pallas_call x1, Pallas kernels, step(): pl.pallas_call(functools.partial(kernel, cfg), out_shape=(out, out), in_s...  36.9 us
    reshape x1, local copies, waits for them, and re-layouts, step(): return tuple((jnp.swapaxes(o, 1, 2).reshape(forcing.shape) for o in outs))  1.61 us

profile of v5, /device:TPU:1, one launch (start us, length us, event | category | flops | bytes accessed | tf_op | source)
XLA Modules:
  0.0 39.2 jit_solution(1790459187439182726)
XLA Ops:
  0.6 36.9 %shard_map.59 = (f32[12,2,96,128]{3,2,1,0:T(8,128)S(1)}, f32[12,2,96,128]{3,2,1,0:T(8,128)S(1)}) custom-call(f32[12]{0:T(128)} %scale_hbm.1, f32[12,96,256]{2,1,0:T(8,128)} %f_hbm.1, f32[96,256]{1,0:T(8,128)} %met_hbm.1, f32[96,256]{1,0:T(8,128)} %jac_hbm.1), custom_call_target="tpu_custom_call" | custom-call | tf_op jit(solution)/shard_map/pallas_call | solution.py:575
  37.6 1.6 %copy_bitcast_fusion = (f32[12,96,256]{2,1,0:T(8,128)}, f32[12,96,256]{2,1,0:T(8,128)}) fusion(f32[12,2,96,128]{3,2,1,0:T(8,128)S(1)} %get-tuple-element.4, f32[12,2,96,128]{3,2,1,0:T(8,128)S(1)} %get-tuple-element.5), kind=kLoop, calls=%fused_computation | loop fusion | bytes 4718592 | tf_op jit(solution)/shard_map/reshape | solution.py:618

commit v6 on v4

--- a/solution.py
+++ b/solution.py
@@ -464,21 +464,24 @@
             send_rows(following, k + 1, side)
         return following
 
+    def gather_dots(first, last):
+        local = jnp.zeros((8, 128), F32)
+        for p in range(n_pairs):
+            stacked = jnp.zeros((8, 128), F32)
+            for q in range(first, last):
+                stacked = jnp.where(subl == q, jnp.sum(dots[q, p], axis=0, keepdims=True), stacked)
+            for par in range(2):
+                half = jnp.where(low_half, stacked, 0.0) if par == 0 else jnp.where(low_half, 0.0, stacked)
+                local = jnp.where(lane == 2 * p + par, jnp.sum(half, axis=1, keepdims=True), local)
+        return local
+
     sent0 = first_exchange()
     sent1 = run_step(0, sent0, w0, w1, None, y0)
     send_cols(sent1, 1, w1)
     sent2 = run_step(1, sent1, w1, w2, y0, y1)
     send_cols(sent2, 2, w2)
+    early = gather_dots(0, 4)
     sent3 = run_step(2, sent2, w2, w3, y1, y2)
-
-    local = jnp.zeros((8, 128), F32)
-    for p in range(n_pairs):
-        stacked = jnp.zeros((8, 128), F32)
-        for q in range(6):
-            stacked = jnp.where(subl == q, jnp.sum(dots[q, p], axis=0, keepdims=True), stacked)
-        for par in range(2):
-            half = jnp.where(low_half, stacked, 0.0) if par == 0 else jnp.where(low_half, 0.0, stacked)
-            local = jnp.where(lane == 2 * p + par, jnp.sum(half, axis=1, keepdims=True), local)
 
     def phase_start(i, value, size, pos, member):
         red[i, pos] = value
@@ -506,7 +509,7 @@
         for p in range(n_pairs):
             to_natural(slot, planes, p)
 
-    moves_a = phase_start(0, local, n_zc, zc_pos, a_member)
+    moves_a = phase_start(0, early + gather_dots(4, 6), n_zc, zc_pos, a_member)
     send_cols(sent3, 3, w3)
     for slot, planes in enumerate((y0, y1, y2)):
         run_natural(slot, planes)

time: 39.4 us -> 39.4 us (level)
  no operation moved by 1% of the time
where the time goes in v6:
time: 39.4 us; the launch traced here: 39.2 us
  Pallas kernels  37 us (94%)
  local copies, waits for them, and re-layouts  1.61 us (4%)
  between operations  0.64 us (2%)
    pallas_call x1, Pallas kernels, step(): pl.pallas_call(functools.partial(kernel, cfg), out_shape=(out, out), in_s...  37 us
    reshape x1, local copies, waits for them, and re-layouts, step(): return tuple((jnp.swapaxes(o, 1, 2).reshape(forcing.shape) for o in outs))  1.61 us

profile of v6, /device:TPU:1, one launch (start us, length us, event | category | flops | bytes accessed | tf_op | source)
XLA Modules:
  0.0 39.2 jit_solution(6762613251133638478)
XLA Ops:
  0.6 37.0 %shard_map.59 = (f32[12,2,96,128]{3,2,1,0:T(8,128)S(1)}, f32[12,2,96,128]{3,2,1,0:T(8,128)S(1)}) custom-call(f32[12]{0:T(128)} %scale_hbm.1, f32[12,96,256]{2,1,0:T(8,128)} %f_hbm.1, f32[96,256]{1,0:T(8,128)} %met_hbm.1, f32[96,256]{1,0:T(8,128)} %jac_hbm.1), custom_call_target="tpu_custom_call" | custom-call | tf_op jit(solution)/shard_map/pallas_call | solution.py:578
  37.6 1.6 %copy_bitcast_fusion = (f32[12,96,256]{2,1,0:T(8,128)}, f32[12,96,256]{2,1,0:T(8,128)}) fusion(f32[12,2,96,128]{3,2,1,0:T(8,128)S(1)} %get-tuple-element.4, f32[12,2,96,128]{3,2,1,0:T(8,128)S(1)} %get-tuple-element.5), kind=kLoop, calls=%fused_computation | loop fusion | bytes 4718592 | tf_op jit(solution)/shard_map/reshape | solution.py:621
